TPU v7x, 128 devices: a whole 4x4x4 slice. The times are simulated.
128 devices in a mesh: scan: 32 (over z, y, core), grp: 4 (over x).
Axes of the slice: x: 4, y: 4, z: 4, core: 2. Of those that a mesh axis runs over, the one named last changes fastest.
Arguments:
- samples: float32 [512, 64, 6, 128], P('scan', 'grp'), may hold values from -6 to 6
- point_count: int32 [512], P('scan'), may hold values from 4096 to 8192
- corr_scan: int32 [512, 64], P('scan', 'grp'), may hold values from 0 to 511, as said below
- corr_tile: int32 [512, 64], P('scan', 'grp'), may hold values from 0 to 63
- corr_src: int32 [512, 64, 128], P('scan', 'grp'), may hold values from 0 to 2047
Outputs:
- hessian: float32 [512, 6, 6, 512], P('scan', None, None, 'grp')
- gradient: float32 [512, 6], P(('scan', 'grp'))
Inputs may be any that keep to these rules, and one draw needn't show every extreme that they name: Never the scan of the entry's own row. A named tile is held by the device with scan index corr_scan // 16 and grp index corr_tile // 16; the 256 entries of one device name at most 4 tiles held by any one device, and in every draw some device is named exactly 4 times by every device.
All inputs are finite; a program needn't handle non-finite values.
Results may differ from a plain program's by a relative error of at most 0.00021.
Values sent between devices are 32-bit elements; how exact they have to be, the bound alone decides.
A program may use at most 64 MiB of HBM per device.

v0:
```python
import jax
import jax.numpy as jnp
from jax import lax
from jax.sharding import PartitionSpec as P


def cut_along(x, dim, length):
    lengths = x.shape
    blocks = x.reshape(*lengths[:dim], length, lengths[dim] // length, *lengths[dim + 1 :])
    return jnp.moveaxis(blocks, dim, 0)


def summed_on_arrival(x, axis, dim):
    length = lax.axis_size(axis)
    blocks = lax.all_to_all(cut_along(x, dim, length), axis, 0, 0, tiled=True)
    return jnp.sum(blocks, axis=0)


def pair_blocks(pos_x, pos_y, pos_z, source_mask, tile_data):
    diff_x = pos_x - tile_data[:, 0, :]
    diff_y = pos_y - tile_data[:, 1, :]
    diff_z = pos_z - tile_data[:, 2, :]
    normal_x = tile_data[:, 3, :]
    normal_y = tile_data[:, 4, :]
    normal_z = tile_data[:, 5, :]
    residual = normal_x * diff_x + normal_y * diff_y + normal_z * diff_z
    weight = source_mask / (1.0 + residual * residual)
    jacobian = jnp.stack(
        [
            pos_y * normal_z - pos_z * normal_y,
            pos_z * normal_x - pos_x * normal_z,
            pos_x * normal_y - pos_y * normal_x,
            normal_x,
            normal_y,
            normal_z,
        ],
        axis=1,
    )
    blocks = jnp.einsum(
        "nik,njk->nij", jacobian * weight[:, None, :], jacobian, precision=lax.Precision.HIGHEST
    )
    vectors = jnp.einsum("nik,nk->ni", jacobian, weight * residual, precision=lax.Precision.HIGHEST)
    return (blocks.reshape(-1, 36), vectors)


def pick_points(samples, point_ids):
    scan_local = samples.shape[0]
    tiles_local = samples.shape[1]
    group_points = tiles_local * 128
    pick_total = point_ids.shape[1]
    block = pick_total
    while block > 128 and block % 2 == 0 and (group_points * block > 4194304):
        block = block // 2
    positions = samples[:, :, 0:3, :].transpose(0, 2, 1, 3).reshape(scan_local, 3, group_points)
    point_iota = jnp.arange(group_points, dtype=jnp.int32)[:, None]

    def one_scan(operands):
        position, picks = operands
        picks = picks.reshape(pick_total // block, block)

        def one_block(wanted):
            selector = (point_iota == wanted[None, :]).astype(jnp.float32)
            return jnp.dot(
                position,
                selector,
                precision=lax.Precision.HIGHEST,
                preferred_element_type=jnp.float32,
            )

        chosen = lax.map(one_block, picks)
        return chosen.transpose(1, 0, 2).reshape(3, pick_total)

    picked = lax.map(one_scan, (positions, point_ids))
    return picked.transpose(1, 0, 2).reshape(3, -1, 128)


def masked_tiles(samples, point_count, codes, group_index):
    tiles_local = samples.shape[1]
    safe_codes = jnp.maximum(codes, 0)
    scan_local = safe_codes // tiles_local
    tile_local = safe_codes % tiles_local
    tile_table = samples.reshape(-1, 6, 128)
    picked = tile_table[safe_codes]
    limits = point_count[scan_local]
    point_ids = (group_index * tiles_local + tile_local)[..., None] * 128 + jnp.arange(128)
    valid_rows = (point_ids < limits[..., None]).astype(jnp.float32)
    return jnp.concatenate(
        [picked[..., 0:3, :], picked[..., 3:6, :] * valid_rows[..., None, :]], axis=-2
    )


def assemble(row_ids, own_scan, other_scan, blocks, vectors, row_count, column_count):
    row_hot = (row_ids[:, None] == jnp.arange(row_count)[None, :]).astype(jnp.float32)
    columns = jnp.arange(column_count)
    column_mix = (own_scan[:, None] == columns[None, :]).astype(jnp.float32) - (
        other_scan[:, None] == columns[None, :]
    ).astype(jnp.float32)
    weighted = (row_hot[:, :, None] * blocks[:, None, :]).reshape(blocks.shape[0], row_count * 36)
    hessian = jnp.einsum(
        "sk,sc->kc", weighted, column_mix, precision=lax.Precision.HIGHEST
    ).reshape(row_count, 6, 6, column_count)
    gradient = jnp.einsum("sl,sj->lj", row_hot, vectors, precision=lax.Precision.HIGHEST)
    return (hessian, gradient)


def local(samples, point_count, corr_scan, corr_tile, corr_src):
    scan_local = samples.shape[0]
    tiles_local = samples.shape[1]
    per_scan = corr_scan.shape[1]
    request_count = scan_local * per_scan
    device_count = lax.axis_size(("scan", "grp"))
    group_count = lax.axis_size("grp")
    slot_cap = 2 * request_count // device_count
    scan_index = lax.axis_index("scan")
    group_index = lax.axis_index("grp")
    scan_total = scan_local * lax.axis_size("scan")
    group_points = tiles_local * 128
    point_ids = corr_src.reshape(scan_local, per_scan * 128)
    picked = pick_points(samples, point_ids)
    coords = [picked[0], picked[1], picked[2]]
    source_mask = (
        (group_index * group_points + point_ids < point_count[:, None])
        .astype(jnp.float32)
        .reshape(request_count, 128)
    )
    target_scan = corr_scan.reshape(-1)
    target_tile = corr_tile.reshape(-1)
    destination = target_scan // scan_local * group_count + target_tile // tiles_local
    codes = target_scan % scan_local * tiles_local + target_tile % tiles_local
    onehot = (destination[:, None] == jnp.arange(device_count)[None, :]).astype(jnp.int32)
    earlier = jnp.cumsum(onehot, axis=0) - onehot
    slot_rank = jnp.sum(earlier * onehot, axis=1)
    slot_ids = destination * slot_cap + slot_rank
    source_scan = scan_index * scan_local + jnp.arange(request_count) // per_scan
    request_ids = jnp.full((device_count * slot_cap, 2), -1, jnp.int32)
    request_ids = (
        request_ids.at[slot_ids]
        .set(jnp.stack([codes, source_scan], axis=1))
        .reshape(device_count, slot_cap, 2)
    )
    payload = jnp.stack(coords + [source_mask], axis=1)
    sent_points = (
        jnp.zeros((device_count * slot_cap, 4, 128), jnp.float32)
        .at[slot_ids]
        .set(payload)
        .reshape(device_count, slot_cap, 4, 128)
    )
    points = lax.all_to_all(sent_points, ("scan", "grp"), split_axis=0, concat_axis=0, tiled=True)
    requests = lax.all_to_all(request_ids, ("scan", "grp"), split_axis=0, concat_axis=0, tiled=True)
    lead_shape = requests.shape[:2]
    fetched = masked_tiles(samples, point_count, requests[..., 0], group_index).reshape(-1, 6, 128)
    flat_points = points.reshape(-1, 4, 128)
    blocks, vectors = pair_blocks(
        flat_points[:, 0], flat_points[:, 1], flat_points[:, 2], flat_points[:, 3], fetched
    )
    blocks = blocks.reshape(lead_shape + (36,))
    vectors = vectors.reshape(lead_shape + (6,))
    back_blocks = lax.all_to_all(blocks, ("scan", "grp"), split_axis=0, concat_axis=0, tiled=True)
    back_vectors = lax.all_to_all(vectors, ("scan", "grp"), split_axis=0, concat_axis=0, tiled=True)
    back_blocks, back_vectors, in_blocks, in_vectors, received = (
        back_blocks,
        back_vectors,
        blocks,
        vectors,
        requests,
    )
    out_blocks = back_blocks.reshape(-1, 36)[slot_ids]
    out_vectors = back_vectors.reshape(-1, 6)[slot_ids]
    in_codes = received[..., 0].reshape(-1)
    in_source = received[..., 1].reshape(-1)
    in_local = jnp.maximum(in_codes, 0) // tiles_local
    row_ids = jnp.concatenate([jnp.arange(request_count) // per_scan, in_local])
    own_scan = scan_index * scan_local + row_ids
    other_scan = jnp.concatenate([target_scan, in_source])
    all_blocks = jnp.concatenate([out_blocks, in_blocks.reshape(-1, 36)], axis=0)
    all_vectors = jnp.concatenate([out_vectors, -in_vectors.reshape(-1, 6)], axis=0)
    hess_part, grad_part = assemble(
        row_ids, own_scan, other_scan, all_blocks, all_vectors, scan_local, scan_total
    )
    hessian, gradient = (
        summed_on_arrival(hess_part, "grp", 3),
        summed_on_arrival(grad_part, "grp", 0),
    )
    return (hessian, gradient)


def solution(mesh):
    placed = (
        P("scan", "grp", None, None),
        P("scan"),
        P("scan", "grp"),
        P("scan", "grp"),
        P("scan", "grp", None),
    )
    return jax.shard_map(
        local,
        mesh=mesh,
        in_specs=placed,
        out_specs=(P("scan", None, None, "grp"), P(("scan", "grp"), None)),
        check_vma=False,
    )
```

profile of v0, /device:TPU:1, one launch (start us, length us, event | category | flops | bytes accessed | tf_op | source)
XLA Modules:
  0.0 223.2 jit_solution(17858029855641656181)
XLA Ops:
  9.0 11.5 %all-to-all-start = ((s32[128,4,2]{1,2,0:T(2,128)}), s32[128,4,2]{1,2,0:T(2,128)S(1)}, u32[]{:S(2)}, u32[]{:S(2)}) async-start(s32[128,4,2]{1,2,0:T(2,128)} %copy.234), calls=%async_computation | async-start | bytes 262144 | tf_op jit(solution)/shard_map/all_to_all | solution.py:149
  21.5 83.6 %while.11 = (s32[]{:T(128)}, f32[16,3,2048]{2,1,0:T(4,128)S(1)}, f32[16,3,2048]{2,1,0:T(4,128)S(1)}, s32[16,2048]{1,0:T(8,128)S(1)}, s32[]{:T(128)}) while((s32[]{:T(128)}, f32[16,3,2048]{2,1,0:T(4,128)S(1)}, f32[16,3,2048]{2,1,0:T(4,128)S(1)}, s32[16,2048]{1,0:T(8,128)S(1)}, s32[]{:T(128)}) %tuple.65), condition=%wide.region_5.6_spmd.clone, body=%wide.region_4.5_spmd.clone.sunk | while | flops 155189248 | bytes 91201 | solution.py:73
  21.5 5.2 %fusion.78 = f32[16,3,2048]{2,1,0:T(4,128)S(1)} fusion(f32[16,3,2048]{2,1,0:T(4,128)S(1)} %get-tuple-element.157, s32[]{:T(128)} %get-tuple-element.156, s32[2048]{0:T(1024)S(1)} %bitcast.176, f32[16,3,2048]{2,1,0:T(4,128)S(1)} %get-tuple-element.163), kind=kOutput, calls=%fused_computation.10.clone.1 | convolution fusion | flops 155189248 | bytes 74752 | tf_op jit(solution)/shard_map/while/body/eval_jaxpr/while/body/eval_jaxpr/dot_general | solution.py:63
  26.7 5.2 %fusion.78 = f32[16,3,2048]{2,1,0:T(4,128)S(1)} fusion(f32[16,3,2048]{2,1,0:T(4,128)S(1)} %get-tuple-element.157, s32[]{:T(128)} %get-tuple-element.156, s32[2048]{0:T(1024)S(1)} %bitcast.176, f32[16,3,2048]{2,1,0:T(4,128)S(1)} %get-tuple-element.163), kind=kOutput, calls=%fused_computation.10.clone.1 | convolution fusion | flops 155189248 | bytes 74752 | tf_op jit(solution)/shard_map/while/body/eval_jaxpr/while/body/eval_jaxpr/dot_general | solution.py:63
  32.0 5.2 %fusion.78 = f32[16,3,2048]{2,1,0:T(4,128)S(1)} fusion(f32[16,3,2048]{2,1,0:T(4,128)S(1)} %get-tuple-element.157, s32[]{:T(128)} %get-tuple-element.156, s32[2048]{0:T(1024)S(1)} %bitcast.176, f32[16,3,2048]{2,1,0:T(4,128)S(1)} %get-tuple-element.163), kind=kOutput, calls=%fused_computation.10.clone.1 | convolution fusion | flops 155189248 | bytes 74752 | tf_op jit(solution)/shard_map/while/body/eval_jaxpr/while/body/eval_jaxpr/dot_general | solution.py:63
  37.2 5.2 %fusion.78 = f32[16,3,2048]{2,1,0:T(4,128)S(1)} fusion(f32[16,3,2048]{2,1,0:T(4,128)S(1)} %get-tuple-element.157, s32[]{:T(128)} %get-tuple-element.156, s32[2048]{0:T(1024)S(1)} %bitcast.176, f32[16,3,2048]{2,1,0:T(4,128)S(1)} %get-tuple-element.163), kind=kOutput, calls=%fused_computation.10.clone.1 | convolution fusion | flops 155189248 | bytes 74752 | tf_op jit(solution)/shard_map/while/body/eval_jaxpr/while/body/eval_jaxpr/dot_general | solution.py:63
  42.4 5.2 %fusion.78 = f32[16,3,2048]{2,1,0:T(4,128)S(1)} fusion(f32[16,3,2048]{2,1,0:T(4,128)S(1)} %get-tuple-element.157, s32[]{:T(128)} %get-tuple-element.156, s32[2048]{0:T(1024)S(1)} %bitcast.176, f32[16,3,2048]{2,1,0:T(4,128)S(1)} %get-tuple-element.163), kind=kOutput, calls=%fused_computation.10.clone.1 | convolution fusion | flops 155189248 | bytes 74752 | tf_op jit(solution)/shard_map/while/body/eval_jaxpr/while/body/eval_jaxpr/dot_general | solution.py:63
  47.6 5.2 %fusion.78 = f32[16,3,2048]{2,1,0:T(4,128)S(1)} fusion(f32[16,3,2048]{2,1,0:T(4,128)S(1)} %get-tuple-element.157, s32[]{:T(128)} %get-tuple-element.156, s32[2048]{0:T(1024)S(1)} %bitcast.176, f32[16,3,2048]{2,1,0:T(4,128)S(1)} %get-tuple-element.163), kind=kOutput, calls=%fused_computation.10.clone.1 | convolution fusion | flops 155189248 | bytes 74752 | tf_op jit(solution)/shard_map/while/body/eval_jaxpr/while/body/eval_jaxpr/dot_general | solution.py:63
  52.9 5.2 %fusion.78 = f32[16,3,2048]{2,1,0:T(4,128)S(1)} fusion(f32[16,3,2048]{2,1,0:T(4,128)S(1)} %get-tuple-element.157, s32[]{:T(128)} %get-tuple-element.156, s32[2048]{0:T(1024)S(1)} %bitcast.176, f32[16,3,2048]{2,1,0:T(4,128)S(1)} %get-tuple-element.163), kind=kOutput, calls=%fused_computation.10.clone.1 | convolution fusion | flops 155189248 | bytes 74752 | tf_op jit(solution)/shard_map/while/body/eval_jaxpr/while/body/eval_jaxpr/dot_general | solution.py:63
  58.1 5.2 %fusion.78 = f32[16,3,2048]{2,1,0:T(4,128)S(1)} fusion(f32[16,3,2048]{2,1,0:T(4,128)S(1)} %get-tuple-element.157, s32[]{:T(128)} %get-tuple-element.156, s32[2048]{0:T(1024)S(1)} %bitcast.176, f32[16,3,2048]{2,1,0:T(4,128)S(1)} %get-tuple-element.163), kind=kOutput, calls=%fused_computation.10.clone.1 | convolution fusion | flops 155189248 | bytes 74752 | tf_op jit(solution)/shard_map/while/body/eval_jaxpr/while/body/eval_jaxpr/dot_general | solution.py:63
  63.3 5.2 %fusion.78 = f32[16,3,2048]{2,1,0:T(4,128)S(1)} fusion(f32[16,3,2048]{2,1,0:T(4,128)S(1)} %get-tuple-element.157, s32[]{:T(128)} %get-tuple-element.156, s32[2048]{0:T(1024)S(1)} %bitcast.176, f32[16,3,2048]{2,1,0:T(4,128)S(1)} %get-tuple-element.163), kind=kOutput, calls=%fused_computation.10.clone.1 | convolution fusion | flops 155189248 | bytes 74752 | tf_op jit(solution)/shard_map/while/body/eval_jaxpr/while/body/eval_jaxpr/dot_general | solution.py:63
  68.5 5.2 %fusion.78 = f32[16,3,2048]{2,1,0:T(4,128)S(1)} fusion(f32[16,3,2048]{2,1,0:T(4,128)S(1)} %get-tuple-element.157, s32[]{:T(128)} %get-tuple-element.156, s32[2048]{0:T(1024)S(1)} %bitcast.176, f32[16,3,2048]{2,1,0:T(4,128)S(1)} %get-tuple-element.163), kind=kOutput, calls=%fused_computation.10.clone.1 | convolution fusion | flops 155189248 | bytes 74752 | tf_op jit(solution)/shard_map/while/body/eval_jaxpr/while/body/eval_jaxpr/dot_general | solution.py:63
  73.8 5.2 %fusion.78 = f32[16,3,2048]{2,1,0:T(4,128)S(1)} fusion(f32[16,3,2048]{2,1,0:T(4,128)S(1)} %get-tuple-element.157, s32[]{:T(128)} %get-tuple-element.156, s32[2048]{0:T(1024)S(1)} %bitcast.176, f32[16,3,2048]{2,1,0:T(4,128)S(1)} %get-tuple-element.163), kind=kOutput, calls=%fused_computation.10.clone.1 | convolution fusion | flops 155189248 | bytes 74752 | tf_op jit(solution)/shard_map/while/body/eval_jaxpr/while/body/eval_jaxpr/dot_general | solution.py:63
  79.0 5.2 %fusion.78 = f32[16,3,2048]{2,1,0:T(4,128)S(1)} fusion(f32[16,3,2048]{2,1,0:T(4,128)S(1)} %get-tuple-element.157, s32[]{:T(128)} %get-tuple-element.156, s32[2048]{0:T(1024)S(1)} %bitcast.176, f32[16,3,2048]{2,1,0:T(4,128)S(1)} %get-tuple-element.163), kind=kOutput, calls=%fused_computation.10.clone.1 | convolution fusion | flops 155189248 | bytes 74752 | tf_op jit(solution)/shard_map/while/body/eval_jaxpr/while/body/eval_jaxpr/dot_general | solution.py:63
  84.2 5.2 %fusion.78 = f32[16,3,2048]{2,1,0:T(4,128)S(1)} fusion(f32[16,3,2048]{2,1,0:T(4,128)S(1)} %get-tuple-element.157, s32[]{:T(128)} %get-tuple-element.156, s32[2048]{0:T(1024)S(1)} %bitcast.176, f32[16,3,2048]{2,1,0:T(4,128)S(1)} %get-tuple-element.163), kind=kOutput, calls=%fused_computation.10.clone.1 | convolution fusion | flops 155189248 | bytes 74752 | tf_op jit(solution)/shard_map/while/body/eval_jaxpr/while/body/eval_jaxpr/dot_general | solution.py:63
  89.4 5.2 %fusion.78 = f32[16,3,2048]{2,1,0:T(4,128)S(1)} fusion(f32[16,3,2048]{2,1,0:T(4,128)S(1)} %get-tuple-element.157, s32[]{:T(128)} %get-tuple-element.156, s32[2048]{0:T(1024)S(1)} %bitcast.176, f32[16,3,2048]{2,1,0:T(4,128)S(1)} %get-tuple-element.163), kind=kOutput, calls=%fused_computation.10.clone.1 | convolution fusion | flops 155189248 | bytes 74752 | tf_op jit(solution)/shard_map/while/body/eval_jaxpr/while/body/eval_jaxpr/dot_general | solution.py:63
  94.7 5.2 %fusion.78 = f32[16,3,2048]{2,1,0:T(4,128)S(1)} fusion(f32[16,3,2048]{2,1,0:T(4,128)S(1)} %get-tuple-element.157, s32[]{:T(128)} %get-tuple-element.156, s32[2048]{0:T(1024)S(1)} %bitcast.176, f32[16,3,2048]{2,1,0:T(4,128)S(1)} %get-tuple-element.163), kind=kOutput, calls=%fused_computation.10.clone.1 | convolution fusion | flops 155189248 | bytes 74752 | tf_op jit(solution)/shard_map/while/body/eval_jaxpr/while/body/eval_jaxpr/dot_general | solution.py:63
  99.9 5.2 %fusion.78 = f32[16,3,2048]{2,1,0:T(4,128)S(1)} fusion(f32[16,3,2048]{2,1,0:T(4,128)S(1)} %get-tuple-element.157, s32[]{:T(128)} %get-tuple-element.156, s32[2048]{0:T(1024)S(1)} %bitcast.176, f32[16,3,2048]{2,1,0:T(4,128)S(1)} %get-tuple-element.163), kind=kOutput, calls=%fused_computation.10.clone.1 | convolution fusion | flops 155189248 | bytes 74752 | tf_op jit(solution)/shard_map/while/body/eval_jaxpr/while/body/eval_jaxpr/dot_general | solution.py:63
  106.8 7.0 %scatter_fusion = f32[512,4,128]{2,1,0:T(4,128)S(1)} fusion(f32[512,4,128]{2,1,0:T(4,128)S(1)} %broadcast_in_dim.15, s32[256]{0:T(256)S(1)} %bitcast.180, f32[256,4,128]{2,1,0:T(4,128)S(1)} %copy.240), kind=kCustom, calls=%fused_computation.4 | custom fusion | bytes 1573888 | tf_op jit(solution)/shard_map/scatter | solution.py:145
  115.1 10.2 %all-to-all-start.1 = ((f32[128,4,4,128]{3,1,2,0:T(4,128)}), f32[128,4,4,128]{3,1,2,0:T(4,128)}, u32[]{:S(2)}, u32[]{:S(2)}) async-start(f32[128,4,4,128]{3,1,2,0:T(4,128)} %copy.241), calls=%async_computation.1 | async-start | bytes 2097152 | tf_op jit(solution)/shard_map/all_to_all | solution.py:148
  125.6 10.1 %fusion.62 = s32[128,4]{0,1:T(4,128)S(1)} fusion(s32[]{:T(128)} %bitcast.35, s32[]{:T(128)} %bitcast.36, s32[]{:T(128)} %bitcast.37, s32[]{:T(128)} %bitcast.38, s32[]{:T(128)} %bitcast.39, s32[]{:T(128)} %bitcast.41, s32[]{:T(128)} %bitcast.40, s32[]{:T(128)} %bitcast.18, s32[]{:T(128)} %bitcast.20, s32[]{:T(128)} %bitcast.22, s32[]{:T(128)} %bitcast.24, ...), kind=kLoop, calls=%fused_computation.114 | loop fusion | flops 21504 | bytes 4160 | tf_op jit(solution)/shard_map/gather | solution.py:84
  141.2 3.3 %all-to-all-done.1 = f32[128,4,4,128]{3,1,2,0:T(4,128)} async-done(((f32[128,4,4,128]{3,1,2,0:T(4,128)}), f32[128,4,4,128]{3,1,2,0:T(4,128)}, u32[]{:S(2)}, u32[]{:S(2)}) %all-to-all-start.1) | async-done | bytes 1048608 | tf_op jit(solution)/shard_map/all_to_all | solution.py:148
  147.4 4.2 %fusion.9 = f32[512,1,6]{2,1,0:T(1,128)S(1)} fusion(f32[512,128,1]{1,2,0:T(1,128)S(1)} %bitcast.166, f32[512,6,128]{2,0,1:T(8,128)S(1)} %get-tuple-element.95), kind=kOutput, calls=%fused_computation.15 | convolution fusion | flops 4718592 | bytes 1847296 | tf_op jit(solution)/shard_map/nik,nk->ni/dot_general | solution.py:42
  152.3 6.5 %all-to-all-start.4 = ((f32[128,4,6]{2,1,0:T(4,128)}), f32[128,4,6]{2,1,0:T(4,128)S(1)}, u32[]{:S(2)}, u32[]{:S(2)}) async-start(f32[128,4,6]{2,1,0:T(4,128)} %bitcast.164), calls=%async_computation.4 | async-start | bytes 524288 | tf_op jit(solution)/shard_map/all_to_all | solution.py:159
  158.8 6.5 %fusion.11 = f32[512,6,6]{2,1,0:T(8,128)} fusion(f32[512,6,128]{2,0,1:T(8,128)S(1)} %get-tuple-element.95, f32[512,6,128]{2,0,1:T(8,128)S(1)} %get-tuple-element.94), kind=kOutput, calls=%fused_computation.17 | convolution fusion | flops 28311552 | bytes 3219456 | tf_op jit(solution)/shard_map/nik,njk->nij/dot_general | solution.py:39
  165.3 2.3 %reshape_reshape.4 = f32[128,4,36]{2,1,0:T(4,128)S(1)} reshape(f32[512,6,6]{2,1,0:T(8,128)} %fusion.11) | data formatting | bytes 147456 | tf_op jit(solution)/shard_map/reshape;reshape | solution.py:156
  170.1 8.8 %all-to-all-start.2 = ((f32[128,1,144]{2,1,0:T(1,128)}), f32[128,1,144]{2,1,0:T(1,128)S(1)}, u32[]{:S(2)}, u32[]{:S(2)}) async-start(f32[128,1,144]{2,1,0:T(1,128)} %reshape.657), calls=%async_computation.2 | async-start | bytes 262144 | tf_op jit(solution)/shard_map/all_to_all | solution.py:158
  180.5 8.3 %all-to-all-done.2 = f32[128,1,144]{2,1,0:T(1,128)S(1)} async-done(((f32[128,1,144]{2,1,0:T(1,128)}), f32[128,1,144]{2,1,0:T(1,128)S(1)}, u32[]{:S(2)}, u32[]{:S(2)}) %all-to-all-start.2) | async-done | bytes 73760 | tf_op jit(solution)/shard_map/all_to_all | solution.py:158
  188.8 3.5 %all-to-all-start.5 = ((f32[4,4,6]{2,1,0:T(4,128)}), f32[4,4,6]{2,1,0:T(4,128)S(1)}, u32[]{:S(2)}, u32[]{:S(2)}) async-start(f32[4,4,6]{2,1,0:T(4,128)} %bitcast.58), calls=%async_computation.5 | async-start | bytes 16384 | tf_op jit(solution)/shard_map/all_to_all | solution.py:15
  197.9 4.0 %fusion.22 = f32[4,16,6,6,128]{4,1,0,3,2:T(8,128)S(1)} fusion(f32[16,6,6,768,1]{3,2,1,0,4:T(8,128)S(1)} %bitcast.165, s32[768]{0:T(1024)S(1)} %pad_add_fusion.1, s32[4,128]{1,0:T(4,128)S(1)} %multiply_add_fusion, s32[768]{0:T(1024)S(1)} %get-tuple-element.102), kind=kOutput, calls=%fused_computation.30 | convolution fusion | flops 2719875072 | bytes 2957312 | tf_op jit(solution)/shard_map/sk,sc->kc/dot_general | solution.py:99
  203.1 3.9 %all-to-all-start.3 = ((f32[4,16,6,6,128]{4,1,3,2,0:T(8,128)}), f32[4,16,6,6,128]{4,1,3,2,0:T(8,128)S(1)}, u32[]{:S(2)}, u32[]{:S(2)}) async-start(f32[4,16,6,6,128]{4,1,3,2,0:T(8,128)} %copy.255), calls=%async_computation.3 | async-start | bytes 2359296 | tf_op jit(solution)/shard_map/all_to_all | solution.py:15
  207.7 14.8 %all-to-all-done.3 = f32[4,16,6,6,128]{4,1,3,2,0:T(8,128)S(1)} async-done(((f32[4,16,6,6,128]{4,1,3,2,0:T(8,128)}), f32[4,16,6,6,128]{4,1,3,2,0:T(8,128)S(1)}, u32[]{:S(2)}, u32[]{:S(2)}) %all-to-all-start.3) | async-done | bytes 1179680 | tf_op jit(solution)/shard_map/all_to_all | solution.py:15
  (121 shorter events, 33.9 us)
Async XLA Ops:
  0.6 19.9 %copy-start.5 = (s32[16]{0:T(128)S(1)}, s32[16]{0:T(128)}, u32[]{:S(2)}) copy-start(s32[16]{0:T(128)} %param.8) | copy-start | bytes 196
  0.6 20.6 %copy-start.3 = (f32[16,16,6,128]{3,1,2,0:T(8,128)S(1)}, f32[16,16,6,128]{3,1,2,0:T(8,128)}, u32[]{:S(2)}) copy-start(f32[16,16,6,128]{3,1,2,0:T(8,128)} %param.7) | copy-start | bytes 2359300
  5.8 15.6 %copy-start.4 = (s32[16,16,128]{2,1,0:T(8,128)S(1)}, s32[16,16,128]{2,1,0:T(8,128)}, u32[]{:S(2)}) copy-start(s32[16,16,128]{2,1,0:T(8,128)} %param.11) | copy-start | bytes 393220
  9.0 106.1 %all-to-all-start = ((s32[128,4,2]{1,2,0:T(2,128)}), s32[128,4,2]{1,2,0:T(2,128)S(1)}, u32[]{:S(2)}, u32[]{:S(2)}) async-start(s32[128,4,2]{1,2,0:T(2,128)} %copy.234), calls=%async_computation | async-start | bytes 262144 | tf_op jit(solution)/shard_map/all_to_all | solution.py:149
  115.1 29.4 %all-to-all-start.1 = ((f32[128,4,4,128]{3,1,2,0:T(4,128)}), f32[128,4,4,128]{3,1,2,0:T(4,128)}, u32[]{:S(2)}, u32[]{:S(2)}) async-start(f32[128,4,4,128]{3,1,2,0:T(4,128)} %copy.241), calls=%async_computation.1 | async-start | bytes 2097152 | tf_op jit(solution)/shard_map/all_to_all | solution.py:148
  146.0 1.1 copy-start.1
  151.6 0.7 copy-start.2
  152.3 17.8 %all-to-all-start.4 = ((f32[128,4,6]{2,1,0:T(4,128)}), f32[128,4,6]{2,1,0:T(4,128)S(1)}, u32[]{:S(2)}, u32[]{:S(2)}) async-start(f32[128,4,6]{2,1,0:T(4,128)} %bitcast.164), calls=%async_computation.4 | async-start | bytes 524288 | tf_op jit(solution)/shard_map/all_to_all | solution.py:159
  165.3 2.3 %copy-start = (f32[512,6,6]{2,1,0:T(8,128)S(1)}, f32[512,6,6]{2,1,0:T(8,128)}, u32[]{:S(2)}) copy-start(f32[512,6,6]{2,1,0:T(8,128)} %fusion.11) | copy-start | bytes 221188
  170.1 18.6 %all-to-all-start.2 = ((f32[128,1,144]{2,1,0:T(1,128)}), f32[128,1,144]{2,1,0:T(1,128)S(1)}, u32[]{:S(2)}, u32[]{:S(2)}) async-start(f32[128,1,144]{2,1,0:T(1,128)} %reshape.657), calls=%async_computation.2 | async-start | bytes 262144 | tf_op jit(solution)/shard_map/all_to_all | solution.py:158
  188.8 14.3 %all-to-all-start.5 = ((f32[4,4,6]{2,1,0:T(4,128)}), f32[4,4,6]{2,1,0:T(4,128)S(1)}, u32[]{:S(2)}, u32[]{:S(2)}) async-start(f32[4,4,6]{2,1,0:T(4,128)} %bitcast.58), calls=%async_computation.5 | async-start | bytes 16384 | tf_op jit(solution)/shard_map/all_to_all | solution.py:15
  203.1 19.3 %all-to-all-start.3 = ((f32[4,16,6,6,128]{4,1,3,2,0:T(8,128)}), f32[4,16,6,6,128]{4,1,3,2,0:T(8,128)S(1)}, u32[]{:S(2)}, u32[]{:S(2)}) async-start(f32[4,16,6,6,128]{4,1,3,2,0:T(8,128)} %copy.255), calls=%async_computation.3 | async-start | bytes 2359296 | tf_op jit(solution)/shard_map/all_to_all | solution.py:15
where the time goes:
time: 225 us; the launch traced here: 223 us
  matrix products  98.8 us (44%)
  starting transfers between devices  44.5 us (20%)
  local copies, waits for them, and re-layouts  36.7 us (16%)
  waiting for transfers between devices  27.3 us (12%)
  other arithmetic  14.7 us (7%)
    dot_general x16, matrix products, one_block(): jnp.dot(position, selector, precision=lax.Precision.HIGHEST, preferred_el...  83.2 us
    all_to_all x2, waiting for transfers between devices, summed_on_arrival(): blocks = lax.all_to_all(cut_along(x, dim, length), axis, 0, 0, tiled=True)  14.8 us
    all_to_all x1, starting transfers between devices, local(): lax.all_to_all(request_ids, ('scan', 'grp'), split_axis=0, concat_axis=0,...  11.5 us
    all_to_all x1, starting transfers between devices, local(): lax.all_to_all(sent_points, ('scan', 'grp'), split_axis=0, concat_axis=0,...  10.2 us
    gather x1, other arithmetic, masked_tiles(): limits = point_count[scan_local]  10.1 us
    all_to_all x1, starting transfers between devices, local(): lax.all_to_all(blocks, ('scan', 'grp'), split_axis=0, concat_axis=0, tile...  8.79 us
    all_to_all x1, waiting for transfers between devices, local(): lax.all_to_all(blocks, ('scan', 'grp'), split_axis=0, concat_axis=0, tile...  8.26 us
    all_to_all x2, starting transfers between devices, summed_on_arrival(): blocks = lax.all_to_all(cut_along(x, dim, length), axis, 0, 0, tiled=True)  7.45 us
  transfers between devices with their start and end apart: 6, of which 4 were waited for; matrix products, arithmetic and copies ran while one was open for 60% of the time, Pallas kernels for 0%

commit v1 on v0

v1 whole, which is shorter than its diff:
```python
import functools

import jax
import jax.numpy as jnp
from jax import lax
from jax.experimental import pallas as pl
from jax.experimental.pallas import tpu as pltpu
from jax.sharding import PartitionSpec as P

F32 = jnp.float32
BF16 = jnp.bfloat16
I32 = jnp.int32
MESH = pl.DeviceIdType.MESH

NS = 32
NG = 4
ND = NS * NG
LOC = 16
TL = 16
CT = 16
REQ = LOC * CT
CAP = 4
STRIDE = 16
USED = 13
FAR = 1000.0
LANES = 128
PAIRS = [(i, j) for i in range(6) for j in range(i, 6)]
PAIR_AT = {}
for _n, (_i, _j) in enumerate(PAIRS):
    PAIR_AT[(_i, _j)] = _n
    PAIR_AT[(_j, _i)] = _n
SUMS = 27
L_SRC, L_DST, L_TILE = 27, 28, 29


def iota(shape, dim):
    return lax.broadcasted_iota(I32, shape, dim)


def dot(a, b):
    return lax.dot_general(a, b, (((1,), (0,)), ((), ())), preferred_element_type=F32)


def parts_of(x, count):
    terms = []
    for _ in range(count):
        term = x.astype(BF16)
        terms.append(term)
        x = x - term.astype(F32)
    return terms


def onehot(cond):
    return jnp.where(cond, 1.0, 0.0).astype(BF16)


def pick_points(pc_ref, src_ref, sm_ref, pay_ref, group):
    first = group * (TL * LANES)

    @pl.loop(0, LOC)
    def _(s):
        picks = src_ref[s]
        tile = lax.shift_right_logical(picks, 7)
        lane = lax.bitwise_and(picks, 127)
        acc = [jnp.zeros((CT, LANES), F32) for _ in range(3)]
        for t in range(TL):
            here = tile == t
            for x in range(3):
                row = jnp.broadcast_to(sm_ref[s, t, pl.ds(x, 1), :], (CT, LANES))
                got = jnp.take_along_axis(row, lane, axis=1, mode="promise_in_bounds")
                acc[x] = jnp.where(here, got, acc[x])
        acc[0] = jnp.where(first + picks < pc_ref[s], acc[0], FAR)
        at = pl.multiple_of(s * CT, CT)
        for x in range(3):
            for n, term in enumerate(parts_of(acc[x], 3)):
                pay_ref[pl.ds(n * REQ + at, CT), x * LANES : (x + 1) * LANES] = term


def pack(cs_ref, ct_ref, pay_ref, msg_ref):
    cs = cs_ref[...]
    ct = ct_ref[...]
    dest = (lax.shift_right_logical(cs, 4) * NG + lax.shift_right_logical(ct, 4)).astype(F32)
    code = (lax.bitwise_and(cs, 15) * TL + lax.bitwise_and(ct, 15) + 1).astype(F32)
    wide = dot(dest.astype(BF16), onehot(iota((CT, REQ), 1) % CT == iota((CT, REQ), 0)))
    wide = jnp.where(iota((LOC, REQ), 1) // CT == iota((LOC, REQ), 0), wide, 0.0)
    dest_t = dot(jnp.ones((ND, LOC), BF16), wide.astype(BF16))
    to_me = dest_t == iota((ND, REQ), 0).astype(F32)
    rank = dot(onehot(to_me), onehot(iota((REQ, REQ), 0) < iota((REQ, REQ), 1)))
    takes = [onehot(to_me & (rank == float(r))) for r in range(CAP)]
    tall = dot(onehot(iota((REQ, LOC), 0) // CT == iota((REQ, LOC), 1)), code.astype(BF16))
    tall = jnp.where(iota((REQ, CT), 0) % CT == iota((REQ, CT), 1), tall, 0.0)
    code_b = dot(tall.astype(BF16), jnp.ones((CT, LANES), BF16))
    place = iota((REQ, LANES), 1) % 32
    target = lax.shift_right_logical(code_b.astype(I32) - 1, 4).astype(F32)
    source = (iota((REQ, LANES), 0) // CT).astype(F32)
    codes = jnp.where(place == L_SRC, source, 0.0)
    codes = jnp.where(place == L_DST, target, codes)
    codes = jnp.where(place == L_TILE, code_b, codes).astype(BF16)
    slot_of_lane = iota((ND, LANES), 1) // 32
    row = jnp.zeros((ND, LANES), F32)
    for r in range(CAP):
        row = jnp.where(slot_of_lane == r, dot(takes[r], codes), row)
    msg_ref[pl.ds(12, ND, stride=STRIDE), :] = row
    for r in range(CAP):
        got = dot(jnp.concatenate([takes[r]] * 3, axis=1), pay_ref[...])
        for x in range(3):
            msg_ref[pl.ds(x * CAP + r, ND, stride=STRIDE), :] = got[:, x * LANES : (x + 1) * LANES]


def pack_kernel(pc_ref, cs_ref, ct_ref, src_ref, sm_ref, msg_ref, pay_ref):
    pick_points(pc_ref, src_ref, sm_ref, pay_ref, lax.axis_index("grp"))
    pack(cs_ref, ct_ref, pay_ref, msg_ref)


def where_is(device):
    return (device // NG, device % NG)


def exchange_kernel(msg_ref, out_ref, send_sem, recv_sem, own_sem):
    me = lax.axis_index("scan") * NG + lax.axis_index("grp")
    barrier = pltpu.get_barrier_semaphore()

    @pl.loop(1, ND)
    def _(step):
        pl.semaphore_signal(barrier, inc=1, device_id=where_is((me + step) % ND), device_id_type=MESH)

    own = pltpu.make_async_copy(
        msg_ref.at[pl.ds(me * STRIDE, STRIDE)], out_ref.at[pl.ds(me * STRIDE, STRIDE)], own_sem
    )
    own.start()
    pl.semaphore_wait(barrier, ND - 1)

    def copy(to, sem_from):
        return pltpu.make_async_remote_copy(
            src_ref=msg_ref.at[pl.ds(to * STRIDE, STRIDE)],
            dst_ref=out_ref.at[pl.ds(sem_from * STRIDE, STRIDE)],
            send_sem=send_sem.at[to],
            recv_sem=recv_sem.at[sem_from],
            device_id=where_is(to),
            device_id_type=MESH,
        )

    @pl.loop(1, ND)
    def _(step):
        copy((me + step) % ND, me).start()

    @pl.loop(1, ND)
    def _(step):
        other = (me + step) % ND
        copy(other, me).wait_send()
        copy(other, other).wait_recv()

    own.wait()


def tile_table(pc_ref, sm_ref, rows_ref, table_ref, group):
    for s in range(LOC):
        for t in range(TL):
            rows_ref[pl.ds((s * TL + t) * 8, 6), :] = sm_ref[s, t]
    point = (group * TL + iota((TL, LANES), 0)) * LANES + iota((TL, LANES), 1)

    @pl.loop(0, LOC)
    def _(s):
        valid = point < pc_ref[s]
        at = pl.multiple_of(s * TL, TL)
        for x in range(6):
            value = rows_ref[pl.ds(s * TL * 8 + x, TL, stride=8), :]
            if x >= 3:
                value = jnp.where(valid, value, 0.0)
            for n, term in enumerate(parts_of(value, 3)):
                table_ref[pl.ds(n * LOC * TL + at, TL), x * LANES : (x + 1) * LANES] = term


def fetch_tiles(msg_ref, table_ref, got_ref):
    codes = msg_ref[pl.ds(12, ND, stride=STRIDE), :]
    for r in range(CAP):
        lane = r * 32 + L_TILE
        wanted = jnp.broadcast_to(codes[:, lane : lane + 1], (ND, LOC * TL))
        take = onehot(wanted == (iota((ND, LOC * TL), 1) + 1).astype(F32))
        got_ref[pl.ds(r * ND, ND), :] = dot(jnp.concatenate([take] * 3, axis=1), table_ref[...])


def tile_sums(msg_ref, got_ref, sums_ref):
    @pl.loop(0, ND // 8)
    def _(block):
        lane = iota((8, LANES), 1)
        at = pl.multiple_of(block * 8, 8)
        bits = [lax.bitwise_and(lane, 1 << b) == 0 for b in range(7)]

        def combine(a, b, level):
            if a is None and b is None:
                return None
            clear = bits[level]
            if b is None:
                return jnp.where(clear, a, 0.0) + pltpu.roll(jnp.where(clear, 0.0, a), 1 << level, 1)
            return jnp.where(clear, a, b) + pltpu.roll(jnp.where(clear, b, a), 1 << level, 1)

        def tree(make, first, count_log, level0):
            if count_log == 0:
                return make(first)
            step = 1 << (count_log - 1)
            return combine(
                tree(make, first, count_log - 1, level0),
                tree(make, first + step, count_log - 1, level0),
                level0 + count_log - 1,
            )

        def slot(r):
            p = [msg_ref[pl.ds(block * (8 * STRIDE) + x * CAP + r, 8, stride=STRIDE), :] for x in range(3)]
            tile = [got_ref[pl.ds(r * ND + at, 8), x * LANES : (x + 1) * LANES] for x in range(6)]
            counts = p[0] < 0.5 * FAR
            p[0] = jnp.where(counts, p[0], 0.0)
            n = tile[3:]
            res = n[0] * (p[0] - tile[0]) + n[1] * (p[1] - tile[1]) + n[2] * (p[2] - tile[2])
            w = jnp.where(counts, 1.0 / (1.0 + res * res), 0.0)
            jac = [
                p[1] * n[2] - p[2] * n[1],
                p[2] * n[0] - p[0] * n[2],
                p[0] * n[1] - p[1] * n[0],
                n[0],
                n[1],
                n[2],
            ]
            wj = [w * j for j in jac]

            def make(k):
                if k < 21:
                    i, j = PAIRS[k]
                    return wj[i] * jac[j]
                if k < SUMS:
                    return wj[k - 21] * res
                return None

            return tree(make, 0, 5, 0)

        total = tree(slot, 0, 2, 5)
        codes = msg_ref[pl.ds(block * (8 * STRIDE) + 12, 8, stride=STRIDE), :]
        sums_ref[pl.ds(at, 8), :] = jnp.where(lax.bitwise_and(lane, 31) < SUMS, total, codes)


def sums_kernel(pc_ref, sm_ref, msg_ref, sums_ref, rows_ref, table_ref, got_ref):
    tile_table(pc_ref, sm_ref, rows_ref, table_ref, lax.axis_index("grp"))
    fetch_tiles(msg_ref, table_ref, got_ref)
    tile_sums(msg_ref, got_ref, sums_ref)


def row_sums(out_rows, in_rows):
    lane = iota((LOC, LANES), 1)
    total = jnp.zeros((LOC, LANES), F32)
    for rows, place, sign in ((out_rows, L_SRC, 1.0), (in_rows, L_DST, -1.0)):
        turned = jnp.transpose(rows)
        hot = jnp.concatenate(
            [
                onehot(jnp.broadcast_to(turned[r * 32 + place : r * 32 + place + 1, :], (LOC, ND)) == iota((LOC, ND), 0).astype(F32))
                for r in range(CAP)
            ],
            axis=0,
        )
        each = sum(dot(hot, term) for term in parts_of(rows, 3))
        part = jnp.zeros((LOC, LANES), F32)
        for r in range(CAP):
            part = jnp.where(lane // 32 == r, each[r * LOC : (r + 1) * LOC], part)
        total = total + jnp.where(lax.bitwise_and(lane, 31) < 21, part, sign * part)
    return total


def return_kernel(sums_ref, out_ref, in_ref, part_ref, send_a, recv_a, send_b, recv_b, send_c, recv_c, own_sem):
    row = lax.axis_index("scan")
    col = lax.axis_index("grp")
    barrier = pltpu.get_barrier_semaphore()
    home = row // 8
    lone = home == col

    @pl.loop(0, 32)
    def _(n):
        src_row = 8 * col + n // NG
        src_col = n % NG

        @pl.when(jnp.logical_or(src_row != row, src_col != col))
        def _():
            pl.semaphore_signal(barrier, inc=1, device_id=(src_row, src_col), device_id_type=MESH)

    for step in range(1, NG):
        pl.semaphore_signal(barrier, inc=1, device_id=(row, (col + step) % NG), device_id_type=MESH)
    pl.semaphore_wait(barrier, 32 + 3 - jnp.where(lone, 1, 0))

    def copy_a(to_row, slot):
        return pltpu.make_async_remote_copy(
            src_ref=sums_ref.at[to_row],
            dst_ref=out_ref.at[slot],
            send_sem=send_a.at[to_row],
            recv_sem=recv_a.at[slot],
            device_id=(to_row, home),
            device_id_type=MESH,
        )

    def copy_b(to_col, slot):
        return pltpu.make_async_remote_copy(
            src_ref=sums_ref.at[pl.ds(to_col * 8, 8)],
            dst_ref=in_ref.at[slot],
            send_sem=send_b.at[to_col],
            recv_sem=recv_b.at[slot],
            device_id=(row, to_col),
            device_id_type=MESH,
        )

    def copy_c(to_col, slot):
        return pltpu.make_async_remote_copy(
            src_ref=part_ref.at[col],
            dst_ref=part_ref.at[slot],
            send_sem=send_c.at[to_col],
            recv_sem=recv_c.at[slot],
            device_id=(row, to_col),
            device_id_type=MESH,
        )

    my_slot = (row % 8) * NG + col
    own_a = pltpu.make_async_copy(sums_ref.at[row], out_ref.at[my_slot], own_sem.at[0])
    own_b = pltpu.make_async_copy(sums_ref.at[pl.ds(col * 8, 8)], in_ref.at[col], own_sem.at[1])
    own_b.start()

    @pl.when(lone)
    def _():
        own_a.start()

    @pl.when(jnp.logical_not(lone))
    def _():
        copy_a(row, my_slot).start()

    @pl.loop(1, NS)
    def _(step):
        copy_a((row + step) % NS, my_slot).start()

    for step in range(1, NG):
        copy_b((col + step) % NG, col).start()

    @pl.loop(0, 32)
    def _(n):
        src_row = 8 * col + n // NG
        src_col = n % NG

        @pl.when(jnp.logical_or(src_row != row, src_col != col))
        def _():
            copy_a(row, n).wait_recv()

    @pl.when(lone)
    def _():
        own_a.wait()

    for step in range(1, NG):
        copy_b(col, (col + step) % NG).wait_recv()
    own_b.wait()

    part_ref[col] = row_sums(out_ref[...].reshape(ND, LANES), in_ref[...].reshape(ND, LANES))
    for step in range(1, NG):
        copy_c((col + step) % NG, col).start()

    @pl.when(jnp.logical_not(lone))
    def _():
        copy_a(row, my_slot).wait_send()

    @pl.loop(1, NS)
    def _(step):
        copy_a((row + step) % NS, my_slot).wait_send()

    for step in range(1, NG):
        copy_b((col + step) % NG, col).wait_send()
        copy_c((col + step) % NG, col).wait_send()
        copy_c(col, (col + step) % NG).wait_recv()


def build_kernel(out_ref, in_ref, part_ref, hess_ref, grad_ref, lhs_ref, rhs_ref):
    row = lax.axis_index("scan")
    col = lax.axis_index("grp")
    rows = [out_ref[...], in_ref[...], part_ref[...].reshape(NG * LOC, LANES)]
    rows[2] = jnp.concatenate([rows[2], jnp.zeros((ND - NG * LOC, LANES), F32)], axis=0)
    wide = jnp.concatenate([jnp.transpose(r) for r in rows], axis=1)
    items = 3 * ND
    out_row = iota((CAP * 48, LANES), 0)
    i_of = (out_row % 48) // 8
    j_of = jnp.minimum(out_row % 8, 5)
    low = jnp.minimum(i_of, j_of)
    high = jnp.maximum(i_of, j_of)
    lane_of = low * 6 - (low * (low - 1)) // 2 + (high - low) + 32 * (out_row // 48)
    spread = onehot(lane_of == iota((CAP * 48, LANES), 1))
    values = [dot(spread, term).astype(BF16) for term in parts_of(wide, 2)]
    lane1 = iota((1, ND), 1)
    for r in range(CAP):
        s_at = r * 32 + L_SRC
        b_at = r * 32 + L_DST
        owner = jnp.concatenate(
            [wide[s_at : s_at + 1, :ND], wide[b_at : b_at + 1, ND : 2 * ND], (lane1 % LOC).astype(F32)], axis=1
        )
        for a in range(LOC):
            mine = onehot(owner == float(a))
            for n in range(2):
                lhs_ref[a * 48 : (a + 1) * 48, (n * CAP + r) * items : (n * CAP + r + 1) * items] = (
                    values[n][r * 48 : (r + 1) * 48] * mine
                )
        item = iota((ND, LANES), 0)
        lane = iota((ND, LANES), 1)
        c_out = jnp.broadcast_to(rows[0][:, b_at : b_at + 1], (ND, LANES)) + (16 * (item // 16)).astype(F32)
        c_in = jnp.broadcast_to(rows[1][:, s_at : s_at + 1], (ND, LANES)) + (16 * ((item % 32) // 4)).astype(F32)
        lane_f = lane.astype(F32)
        diag = (lane == item % LOC + LOC * (row % 8)) & (row // 8 == col) & (item < NG * LOC)
        columns = jnp.concatenate(
            [
                jnp.where(c_out == lane_f, -1.0, 0.0),
                jnp.where(c_in == lane_f, -1.0, 0.0),
                jnp.where(diag, 1.0, 0.0),
            ],
            axis=0,
        ).astype(BF16)
        for n in range(2):
            rhs_ref[(n * CAP + r) * items : (n * CAP + r + 1) * items, :] = columns
    block = dot(lhs_ref[...], rhs_ref[...])
    for a in range(LOC):
        for i in range(6):
            at = (a * 6 + i) * 8
            hess_ref[a, i] = block[at : at + 6, :]
    mine = sum(part_ref[n, pl.ds(col * 4, 4), :] for n in range(NG))
    flat = sum(mine[:, r * 32 : (r + 1) * 32] for r in range(CAP))
    grad_ref[...] = flat[:, 21:27]


def vmem(count):
    return [pl.BlockSpec(memory_space=pltpu.VMEM)] * count


def local(samples, point_count, corr_scan, corr_tile, corr_src):
    smem = [pl.BlockSpec(memory_space=pltpu.SMEM)]
    msg = pl.pallas_call(
        pack_kernel,
        out_shape=jax.ShapeDtypeStruct((ND * STRIDE, LANES), F32),
        in_specs=smem + vmem(4),
        out_specs=pl.BlockSpec(memory_space=pltpu.VMEM),
        scratch_shapes=[pltpu.VMEM((3 * REQ, 3 * LANES), BF16)],
        name="pack",
    )(point_count, corr_scan, corr_tile, corr_src, samples)
    recv = pl.pallas_call(
        exchange_kernel,
        out_shape=jax.ShapeDtypeStruct((ND * STRIDE, LANES), F32),
        in_specs=vmem(1),
        out_specs=pl.BlockSpec(memory_space=pltpu.VMEM),
        scratch_shapes=[
            pltpu.SemaphoreType.DMA((ND,)),
            pltpu.SemaphoreType.DMA((ND,)),
            pltpu.SemaphoreType.DMA,
        ],
        compiler_params=pltpu.CompilerParams(collective_id=0, has_side_effects=True),
        name="exchange",
    )(msg)
    sums = pl.pallas_call(
        sums_kernel,
        out_shape=jax.ShapeDtypeStruct((ND, LANES), F32),
        in_specs=smem + vmem(2),
        out_specs=pl.BlockSpec(memory_space=pltpu.VMEM),
        scratch_shapes=[
            pltpu.VMEM((LOC * TL * 8, LANES), F32),
            pltpu.VMEM((3 * LOC * TL, 6 * LANES), BF16),
            pltpu.VMEM((CAP * ND, 6 * LANES), F32),
        ],
        name="sums",
    )(point_count, samples, recv)
    dma = pltpu.SemaphoreType.DMA
    out_rows, in_rows, parts = pl.pallas_call(
        return_kernel,
        out_shape=(
            jax.ShapeDtypeStruct((32, NG, LANES), F32),
            jax.ShapeDtypeStruct((NG, 8, NG, LANES), F32),
            jax.ShapeDtypeStruct((NG, LOC, LANES), F32),
        ),
        in_specs=vmem(1),
        out_specs=tuple(vmem(3)),
        scratch_shapes=[
            dma((NS,)),
            dma((32,)),
            dma((NG,)),
            dma((NG,)),
            dma((NG,)),
            dma((NG,)),
            dma((2,)),
        ],
        compiler_params=pltpu.CompilerParams(collective_id=1, has_side_effects=True),
        name="give_back",
    )(sums.reshape(NS, NG, LANES))
    hessian, gradient = pl.pallas_call(
        build_kernel,
        out_shape=(
            jax.ShapeDtypeStruct((LOC, 6, 6, LANES), F32),
            jax.ShapeDtypeStruct((4, 6), F32),
        ),
        in_specs=vmem(3),
        out_specs=tuple(vmem(2)),
        scratch_shapes=[
            pltpu.VMEM((LOC * 48, 2 * CAP * 3 * ND), BF16),
            pltpu.VMEM((2 * CAP * 3 * ND, LANES), BF16),
        ],
        name="build",
    )(out_rows.reshape(ND, LANES), in_rows.reshape(ND, LANES), parts)
    return hessian, gradient


def solution(mesh):
    placed = (
        P("scan", "grp", None, None),
        P("scan"),
        P("scan", "grp"),
        P("scan", "grp"),
        P("scan", "grp", None),
    )
    return jax.shard_map(
        local,
        mesh=mesh,
        in_specs=placed,
        out_specs=(P("scan", None, None, "grp"), P(("scan", "grp"), None)),
        check_vma=False,
    )
```

time: 225 us -> 77.9 us (0.35)
  matrix products: 98.8 us -> 0 us
  Pallas kernels: 0 us -> 72.7 us
  starting transfers between devices: 44.5 us -> 0 us
  local copies, waits for them, and re-layouts: 36.7 us -> 4.17 us
  waiting for transfers between devices: 27.3 us -> 0 us
  other arithmetic: 14.7 us -> 0 us
    dot_general x20 -> x0, matrix products: 98.8 us -> none  [the longest x16 83.2 us: one_block(): jnp.dot(position, selector, precision=lax.Precision.HIGHEST, preferred_el...]
    pallas_call x0 -> x5, Pallas kernels: none -> 72.7 us  [the longest x1 32.9 us: local(): pl.pallas_call(exchange_kernel, out_shape=jax.ShapeDtypeStruct((ND * STRI...]
    all_to_all x6 -> x0, starting transfers between devices: 44.5 us -> none  [the longest x1 11.5 us: local(): lax.all_to_all(request_ids, ('scan', 'grp'), split_axis=0, concat_axis=0,...]
    all_to_all x6 -> x0, waiting for transfers between devices: 27.3 us -> none  [the longest x2 14.8 us: summed_on_arrival(): blocks = lax.all_to_all(cut_along(x, dim, length), axis, 0, 0, tiled=True)]
    gather x3 -> x0, other arithmetic: 10.1 us -> none  [the longest x1 10.1 us: masked_tiles(): limits = point_count[scan_local]]
    scatter x2 -> x0, local copies, waits for them, and re-layouts: 8.19 us -> none  [the longest x1 6.97 us: local(): sent_points = jnp.zeros((device_count * slot_cap, 4, 128), jnp.float32).a...]
    reshape x10 -> x0, local copies, waits for them, and re-layouts: 8.16 us -> none  [the longest x3 2.41 us: local(): target_scan = corr_scan.reshape(-1)]
    gather x7 -> x0, local copies, waits for them, and re-layouts: 4.33 us -> none  [the longest x1 1.88 us: masked_tiles(): picked = tile_table[safe_codes]]
  transfers between devices with their start and end apart: 6 -> 0, of which waited for: 4 -> 0; matrix products, arithmetic and copies ran while one was open for 60% -> 0% of each run, Pallas kernels for 0% -> 0%
where the time goes in v1:
time: 77.9 us; the launch traced here: 77.5 us
  Pallas kernels  72.7 us (93%)
  local copies, waits for them, and re-layouts  4.17 us (5%)
    pallas_call x1, Pallas kernels, local(): pl.pallas_call(exchange_kernel, out_shape=jax.ShapeDtypeStruct((ND * STRI...  32.9 us
    pallas_call x1, Pallas kernels, local(): pl.pallas_call(return_kernel, out_shape=(jax.ShapeDtypeStruct((32, NG, LA...  17.3 us
    pallas_call x1, Pallas kernels, local(): pl.pallas_call(sums_kernel, out_shape=jax.ShapeDtypeStruct((ND, LANES), F...  12.5 us
    pallas_call x1, Pallas kernels, local(): pl.pallas_call(pack_kernel, out_shape=jax.ShapeDtypeStruct((ND * STRIDE,...  6.57 us
    pallas_call x1, Pallas kernels, local(): pl.pallas_call(build_kernel, out_shape=(jax.ShapeDtypeStruct((LOC, 6, 6,...  3.46 us
    unnamed x1, local copies, waits for them, and re-layouts  2.37 us
    pallas_call x1, local copies, waits for them, and re-layouts, local(): pl.pallas_call(build_kernel, out_shape=(jax.ShapeDtypeStruct((LOC, 6, 6,...  1.81 us

profile of v1, /device:TPU:1, one launch (start us, length us, event | category | flops | bytes accessed | tf_op | source)
XLA Modules:
  0.0 77.5 jit_solution(9148731656317825009)
XLA Ops:
  0.6 2.4 %copy.8.sm_ref = f32[16,16,6,128]{3,2,1,0:T(8,128)} copy(f32[16,16,6,128]{3,1,2,0:T(8,128)} %param.5) | data formatting | bytes 1572864 | tf_op args[0]
  3.0 6.6 %pack.1.msg_ref = f32[2048,128]{1,0:T(8,128)} custom-call(s32[16]{0:T(128)} %pc_ref.3, s32[16,16]{1,0:T(8,128)} %cs_ref.1, s32[16,16]{1,0:T(8,128)} %ct_ref.1, s32[16,16,128]{2,1,0:T(8,128)} %src_ref.1, f32[16,16,6,128]{3,2,1,0:T(8,128)} %copy.8.sm_ref), custom_call_target="tpu_custom_call" | custom-call | tf_op jit(solution)/shard_map/pack/pallas_call | solution.py:432
  9.6 32.9 %exchange.1.msg_ref = f32[2048,128]{1,0:T(8,128)} custom-call(f32[2048,128]{1,0:T(8,128)} %pack.1.msg_ref), custom_call_target="tpu_custom_call" | custom-call | tf_op jit(solution)/shard_map/exchange/pallas_call | solution.py:440
  42.5 12.5 %sums.1 = f32[128,128]{1,0:T(8,128)} custom-call(s32[16]{0:T(128)} %pc_ref.3, f32[16,16,6,128]{3,2,1,0:T(8,128)} %copy.8.sm_ref, f32[2048,128]{1,0:T(8,128)} %exchange.1.msg_ref), custom_call_target="tpu_custom_call" | custom-call | tf_op jit(solution)/shard_map/sums/pallas_call | solution.py:453
  55.0 17.3 %give_back.1 = (f32[32,4,128]{2,1,0:T(4,128)}, f32[4,8,4,128]{3,2,1,0:T(4,128)}, f32[4,16,128]{2,1,0:T(8,128)}) custom-call(f32[32,4,128]{2,1,0:T(4,128)} %bitcast.3), custom_call_target="tpu_custom_call" | custom-call | tf_op jit(solution)/shard_map/give_back/pallas_call | solution.py:466
  72.3 3.5 %build.1 = (f32[16,6,6,128]{3,2,1,0:T(8,128)}, f32[4,6]{1,0:T(4,128)}) custom-call(f32[128,128]{1,0:T(8,128)} %bitcast.4, f32[128,128]{1,0:T(8,128)} %bitcast.5, f32[4,16,128]{2,1,0:T(8,128)} %get-tuple-element.7.part_ref), custom_call_target="tpu_custom_call" | custom-call | tf_op jit(solution)/shard_map/build/pallas_call | solution.py:487
  75.7 1.8 %copy.9 = f32[16,6,6,128]{3,0,2,1:T(8,128)} copy(f32[16,6,6,128]{3,2,1,0:T(8,128)} %get-tuple-element.8) | data formatting | bytes 589824 | tf_op jit(solution)/shard_map/build/pallas_call | solution.py:487

commit v2 on v0

v2 whole, which is shorter than its diff:
```python
import functools

import jax
import jax.numpy as jnp
from jax import lax
from jax.experimental import pallas as pl
from jax.experimental.pallas import tpu as pltpu
from jax.sharding import PartitionSpec as P

F32 = jnp.float32
BF16 = jnp.bfloat16
I32 = jnp.int32
MESH = pl.DeviceIdType.MESH

NS = 32
NG = 4
ND = NS * NG
LOC = 16
TL = 16
CT = 16
REQ = LOC * CT
CAP = 4
ROWS = 13
FAR = 1000.0
LANES = 128
PAIRS = [(i, j) for i in range(6) for j in range(i, 6)]
UNITS = 16
GROUPS = 8
ITEMS = GROUPS * LANES


def iota(shape, dim):
    return lax.broadcasted_iota(I32, shape, dim)


def dot(a, b):
    return lax.dot_general(a, b, (((1,), (0,)), ((), ())), preferred_element_type=F32)


def dot_t(a, b):
    return lax.dot_general(a, b, (((1,), (1,)), ((), ())), preferred_element_type=F32)


def parts_of(x, count):
    terms = []
    for _ in range(count):
        term = x.astype(BF16)
        terms.append(term)
        x = x - term.astype(F32)
    return terms


def onehot(cond):
    return jnp.where(cond, 1.0, 0.0).astype(BF16)


def pick_points(pc_ref, src_ref, sm_ref, pay_ref, group):
    first = group * (TL * LANES)

    @pl.loop(0, LOC)
    def _(s):
        picks = src_ref[s]
        tile = lax.shift_right_logical(picks, 7)
        lane = lax.bitwise_and(picks, 127)
        acc = [jnp.zeros((CT, LANES), F32) for _ in range(3)]
        for t in range(TL):
            here = tile == t
            for x in range(3):
                row = jnp.broadcast_to(sm_ref[s, x, pl.ds(t, 1), :], (CT, LANES))
                got = jnp.take_along_axis(row, lane, axis=1, mode="promise_in_bounds")
                acc[x] = jnp.where(here, got, acc[x])
        acc[0] = jnp.where(first + picks < pc_ref[s], acc[0], FAR)
        at = pl.multiple_of(s * CT, CT)
        for x in range(3):
            for n, term in enumerate(parts_of(acc[x], 3)):
                pay_ref[pl.ds(n * REQ + at, CT), x * LANES : (x + 1) * LANES] = term


def pack(cs_ref, ct_ref, pay_ref, msg_ref, group):
    cs = cs_ref[...]
    ct = ct_ref[...]
    dest = (lax.shift_right_logical(cs, 4) * NG + lax.shift_right_logical(ct, 4)).astype(F32)
    code = (lax.bitwise_and(cs, 15) * TL + lax.bitwise_and(ct, 15) + 1).astype(F32)
    wide = dot(dest.astype(BF16), onehot(iota((CT, REQ), 1) % CT == iota((CT, REQ), 0)))
    wide = jnp.where(iota((LOC, REQ), 1) // CT == iota((LOC, REQ), 0), wide, 0.0)
    dest_t = dot(jnp.ones((ND, LOC), BF16), wide.astype(BF16))
    to_me = dest_t == iota((ND, REQ), 0).astype(F32)
    rank = dot(onehot(to_me), onehot(iota((REQ, REQ), 0) < iota((REQ, REQ), 1)))
    takes = [onehot(to_me & (rank == float(r))) for r in range(CAP)]
    tall = dot(onehot(iota((REQ, LOC), 0) // CT == iota((REQ, LOC), 1)), code.astype(BF16))
    tall = jnp.where(iota((REQ, CT), 0) % CT == iota((REQ, CT), 1), tall, 0.0)
    code_b = dot(tall.astype(BF16), jnp.ones((CT, LANES), BF16))
    target = lax.shift_right_logical(code_b.astype(I32) - 1, 4).astype(F32)
    source = (iota((REQ, LANES), 0) // CT).astype(F32)
    lane = iota((REQ, LANES), 1)
    codes = jnp.where(lane < 32, source, jnp.where(lane < 64, target, code_b)).astype(BF16)
    lane = iota((ND, LANES), 1)
    row = jnp.zeros((ND, LANES), F32)
    for r in range(CAP):
        at = r * 8 + group
        here = (lane == at) | (lane == 32 + at) | (lane == 100 + r * 8)
        row = jnp.where(here, dot(takes[r], codes), row)
    msg_ref[pl.ds(12, ND, stride=ROWS), :] = row
    got = dot(
        jnp.concatenate([jnp.concatenate([take] * 3, axis=1) for take in takes], axis=0), pay_ref[...]
    )
    for r in range(CAP):
        for x in range(3):
            msg_ref[pl.ds(x * CAP + r, ND, stride=ROWS), :] = got[r * ND : (r + 1) * ND, x * LANES : (x + 1) * LANES]


def tile_table(pc_ref, sm_ref, table_ref, group):
    point = (group * TL + iota((TL, LANES), 0)) * LANES + iota((TL, LANES), 1)

    @pl.loop(0, LOC)
    def _(s):
        valid = point < pc_ref[s]
        at = pl.multiple_of(s * TL, TL)
        for x in range(6):
            value = sm_ref[s, x]
            if x >= 3:
                value = jnp.where(valid, value, 0.0)
            for n, term in enumerate(parts_of(value, 3)):
                table_ref[pl.ds(n * LOC * TL + at, TL), x * LANES : (x + 1) * LANES] = term


def unit_sums(at, msg_ref, table_ref, left_ref, right_ref):
    lane = iota((8, LANES), 1)
    sub = iota((8, LANES), 0)
    codes = msg_ref[pl.ds(at + 12, 8, stride=ROWS), :]
    tile_at = (iota((8, LOC * TL), 1) + 1).astype(F32)
    take = jnp.concatenate(
        [
            jnp.where(jnp.broadcast_to(codes[:, 100 + r * 8 : 101 + r * 8], (8, LOC * TL)) == tile_at, 1.0, 0.0)
            for r in range(CAP)
        ],
        axis=0,
    ).astype(BF16)
    tile = dot(jnp.concatenate([take] * 3, axis=1), table_ref[...])
    p = [
        jnp.concatenate([msg_ref[pl.ds(at + x * CAP + r, 8, stride=ROWS), :] for r in range(CAP)], axis=0)
        for x in range(3)
    ]
    q = [tile[:, x * LANES : (x + 1) * LANES] for x in range(3)]
    n = [tile[:, x * LANES : (x + 1) * LANES] for x in range(3, 6)]
    counts = p[0] < 0.5 * FAR
    p[0] = jnp.where(counts, p[0], 0.0)
    res = n[0] * (p[0] - q[0]) + n[1] * (p[1] - q[1]) + n[2] * (p[2] - q[2])
    w = jnp.where(counts, 1.0 / (1.0 + res * res), 0.0)
    jac = [
        p[1] * n[2] - p[2] * n[1],
        p[2] * n[0] - p[0] * n[2],
        p[0] * n[1] - p[1] * n[0],
        n[0],
        n[1],
        n[2],
    ]
    for i in range(6):
        high, low = parts_of(w * jac[i], 2)
        left_ref[i * 32 : (i + 1) * 32, :] = jnp.concatenate([high, high, low], axis=1)
    for j, value in enumerate(jac + [res, jnp.zeros_like(res)]):
        high, low = parts_of(value, 2)
        right_ref[j * 32 : (j + 1) * 32, :] = jnp.concatenate([high, low, high], axis=1)
    every = dot_t(left_ref[...], right_ref[...])
    halves = []
    for half in range(2):
        arrays = []
        for i in range(6):
            kept = jnp.zeros((8, LANES), F32)
            for r in range(CAP):
                block = every[i * 32 + r * 8 : i * 32 + r * 8 + 8, half * LANES : (half + 1) * LANES]
                kept = jnp.where(lane % 32 == r * 8 + sub, block, kept)
            arrays.append(kept)
        arrays += [None, None]
        for level in range(3):
            clear = (sub // (1 << level)) % 2 == 0
            arrays = [fold(arrays[n], arrays[n + 1], clear, 1 << level) for n in range(0, len(arrays), 2)]
        halves.append(arrays[0])
    low, high = halves
    first = (lane // 4) % 2 == 0
    blocks = []
    for c in range(2):
        if c == 0:
            block = jnp.where(first, low, pltpu.roll(high, 4, 1))
        else:
            block = jnp.where(first, pltpu.roll(low, LANES - 4, 1), high)
        code = jnp.sum(jnp.where(sub // 4 == c, codes, 0.0), axis=0, keepdims=True)
        blocks.append(jnp.where(sub == 7, jnp.broadcast_to(code, (8, LANES)), block))
    return blocks


def fold(a, b, clear, shift):
    if a is None:
        return None
    if b is None:
        return jnp.where(clear, a, 0.0) + pltpu.roll(jnp.where(clear, 0.0, a), shift, 0)
    return jnp.where(clear, a, b) + pltpu.roll(jnp.where(clear, b, a), shift, 0)


def turn_groups(load, owner_ref, sums_ref, column_ref):
    lane = iota((8, LANES), 1)
    lane1 = iota((1, LANES), 1)
    which = ((lane1 // 4) % 2) * 4 + ((lane1 // 64) % 2) * 2 + (lane1 // 32) % 2
    for q in range(GROUPS):
        blocks = [load(q, m) for m in range(8)]
        for bit, shift in ((1, 64), (0, 32), (2, 4)):
            clear = (lane // shift) % 2 == 0
            for m in range(8):
                if (m >> bit) % 2 == 0:
                    a, b = blocks[m], blocks[m + (1 << bit)]
                    blocks[m] = jnp.where(clear, a, pltpu.roll(b, shift, 1))
                    blocks[m + (1 << bit)] = jnp.where(clear, pltpu.roll(a, LANES - shift, 1), b)
        source = blocks[0][7:8, :]
        target = blocks[1][7:8, :]
        at = q * LANES
        if q < GROUPS // 2:
            owner = source
            column = target + (16 * (2 * q + which // 4)).astype(F32)
        else:
            owner = target
            column = source + (16 * which).astype(F32)
            blocks[6] = -blocks[6]
        mine = jnp.where(jnp.broadcast_to(owner, (LOC, LANES)) == iota((LOC, LANES), 0).astype(F32), 1.0, 0.0)
        there = jnp.where(jnp.broadcast_to(column, (LANES, LANES)) == iota((LANES, LANES), 0).astype(F32), -1.0, 0.0)
        stack = jnp.concatenate(blocks, axis=0)
        for n, term in enumerate(parts_of(stack, 2)):
            owner_ref[:, n * ITEMS + at : n * ITEMS + at + LANES] = mine.astype(BF16)
            column_ref[:, n * ITEMS + at : n * ITEMS + at + LANES] = there.astype(BF16)
            sums_ref[:, n * ITEMS + at : n * ITEMS + at + LANES] = term


def matrix(owner_ref, sums_ref, column_ref, lhs_ref, block_ref):
    for k, (i, j) in enumerate(PAIRS):
        row = sums_ref[j * 8 + i : j * 8 + i + 1, :]
        lhs_ref[k * LOC : (k + 1) * LOC, :] = jnp.broadcast_to(row, (LOC, 2 * ITEMS)) * owner_ref[...]
    block_ref[...] = dot_t(lhs_ref[...], column_ref[...])


def order(p):
    return 2 * (1 - p % 2) + (p % 2 + p // 2) % 2


def step_kernel(
    pc_ref, cs_ref, ct_ref, src_ref, sm_ref, block_ref, part_ref,
    pay_ref, msg_ref, recv_ref, table_ref, left_ref, right_ref, back_ref, out_ref, in_ref,
    owner_ref, sums_ref, column_ref, lhs_ref,
    send_p, recv_p, send_a, recv_a, send_b, recv_b, send_c, recv_c,
):
    row = lax.axis_index("scan")
    col = lax.axis_index("grp")
    z, y, core = row // 8, (row // 2) % 4, row % 2
    me = row * NG + col
    barrier = pltpu.get_barrier_semaphore()

    @pl.loop(1, ND)
    def _(step):
        other = (me + step) % ND
        pl.semaphore_signal(barrier, inc=1, device_id=(other // NG, other % NG), device_id_type=MESH)

    pick_points(pc_ref, src_ref, sm_ref, pay_ref, col)
    pack(cs_ref, ct_ref, pay_ref, msg_ref, col)
    pl.semaphore_wait(barrier, ND - 1)

    def points(to_row, to_col, at):
        to = to_row * NG + to_col
        return pltpu.make_async_remote_copy(
            src_ref=msg_ref.at[pl.ds(to * ROWS, ROWS)],
            dst_ref=recv_ref.at[pl.ds(at * ROWS, ROWS)],
            send_sem=send_p.at[to],
            recv_sem=recv_p.at[at],
            device_id=(to_row, to_col),
            device_id_type=MESH,
        )

    def each_of_unit(u, sign, act):
        uz = (z + sign * order(u // 4) + 4) % 4
        uy = (y + sign * order(u % 4) + 4) % 4
        for dc in range(2):
            for dx in range(NG):
                there = ((uz * 4 + uy) * 2 + (core + dc) % 2, (col + dx) % NG)
                if dc == 0 and dx == 0:

                    @pl.when(u < UNITS - 1)
                    def _():
                        act(*there)

                else:
                    act(*there)
        return uz * 4 + uy

    own = pltpu.make_async_copy(
        msg_ref.at[pl.ds(me * ROWS, ROWS)], recv_ref.at[pl.ds(me * ROWS, ROWS)], recv_p.at[me]
    )
    own.start()

    @pl.loop(0, UNITS)
    def _(u):
        each_of_unit(u, 1, lambda r, c: points(r, c, me).start())

    tile_table(pc_ref, sm_ref, table_ref, col)

    home = row // 8
    slot = (row % 8) * NG + col

    def give(to_row, at):
        return pltpu.make_async_remote_copy(
            src_ref=back_ref.at[to_row],
            dst_ref=out_ref.at[at],
            send_sem=send_a.at[to_row],
            recv_sem=recv_a.at[at],
            device_id=(to_row, home),
            device_id_type=MESH,
        )

    def share(unit, from_col, at):
        return pltpu.make_async_remote_copy(
            src_ref=back_ref.at[pl.ds(2 * unit, 2)],
            dst_ref=in_ref.at[from_col, pl.ds(2 * at, 2)],
            send_sem=send_b.at[unit],
            recv_sem=recv_b.at[from_col * 4 + at],
            device_id=(row, unit // 4),
            device_id_type=MESH,
        )

    @pl.loop(0, UNITS)
    def _(u):
        unit = each_of_unit(u, -1, lambda r, c: points(r, c, r * NG + c).wait_recv())

        @pl.when(u == UNITS - 1)
        def _():
            own.wait()

        first, second = unit_sums(unit * (8 * ROWS), recv_ref, table_ref, left_ref, right_ref)
        back_ref[2 * unit] = first
        back_ref[2 * unit + 1] = second
        for c in range(2):
            to_row = 2 * unit + c
            lone = jnp.logical_and(to_row == row, home == col)

            @pl.when(jnp.logical_not(lone))
            def _():
                give(to_row, slot).start()

            @pl.when(lone)
            def _():
                pltpu.make_async_copy(back_ref.at[to_row], out_ref.at[slot], recv_a.at[slot]).start()

        @pl.when(unit // 4 != col)
        def _():
            share(unit, col, unit % 4).start()

        @pl.when(unit // 4 == col)
        def _():
            pltpu.make_async_copy(
                back_ref.at[pl.ds(2 * unit, 2)], in_ref.at[col, pl.ds(2 * (unit % 4), 2)], recv_b.at[col * 4 + unit % 4]
            ).start()

    @pl.loop(0, 32)
    def _(n):
        give(row, n).wait_recv()

    @pl.loop(0, UNITS)
    def _(n):
        share(0, n // 4, n % 4).wait_recv()

    def load(q, m):
        return out_ref[q * 8 + m] if q < GROUPS // 2 else in_ref[q - GROUPS // 2, m]

    turn_groups(load, owner_ref, sums_ref, column_ref)
    part = dot_t(owner_ref[...], sums_ref[...])
    part_ref[col] = jnp.concatenate([part, jnp.zeros((LOC, LANES - 64), F32)], axis=1)

    def spread(to_col, at):
        return pltpu.make_async_remote_copy(
            src_ref=part_ref.at[col],
            dst_ref=part_ref.at[at],
            send_sem=send_c.at[to_col],
            recv_sem=recv_c.at[at],
            device_id=(row, to_col),
            device_id_type=MESH,
        )

    for step in range(1, NG):
        spread((col + step) % NG, col).start()

    matrix(owner_ref, sums_ref, column_ref, lhs_ref, block_ref)

    @pl.loop(1, ND)
    def _(step):
        other = (me + step) % ND
        points(other // NG, other % NG, me).wait_send()

    @pl.loop(0, NS)
    def _(n):
        @pl.when(jnp.logical_not(jnp.logical_and(n == row, home == col)))
        def _():
            give(n, slot).wait_send()

    @pl.loop(0, UNITS)
    def _(n):
        @pl.when(n // 4 != col)
        def _():
            share(n, col, n % 4).wait_send()

    for step in range(1, NG):
        other = (col + step) % NG
        spread(other, col).wait_send()
        spread(other, other).wait_recv()


def finish_kernel(block_ref, part_ref, hess_ref, grad_ref):
    row = lax.axis_index("scan")
    col = lax.axis_index("grp")
    total = part_ref[0] + part_ref[1] + part_ref[2] + part_ref[3]
    lane = iota((LOC, LANES), 1)
    diag = (lane == iota((LOC, LANES), 0) + LOC * (row % 8)) & (row // 8 == col)
    for k, (i, j) in enumerate(PAIRS):
        at = j * 8 + i
        value = block_ref[k * LOC : (k + 1) * LOC, :] + jnp.where(
            diag, jnp.broadcast_to(total[:, at : at + 1], (LOC, LANES)), 0.0
        )
        hess_ref[i, j] = value
        if i != j:
            hess_ref[j, i] = value
    some = jnp.zeros((4, LANES), F32)
    for n in range(NG):
        some = jnp.where(col == n, total[n * 4 : (n + 1) * 4, :], some)
    grad_ref[...] = some[:, 48:54]


def vmem(count):
    return [pl.BlockSpec(memory_space=pltpu.VMEM)] * count


def local(samples, point_count, corr_scan, corr_tile, corr_src):
    dma = pltpu.SemaphoreType.DMA
    block, parts = pl.pallas_call(
        step_kernel,
        out_shape=(
            jax.ShapeDtypeStruct((len(PAIRS) * LOC, LANES), F32),
            jax.ShapeDtypeStruct((NG, LOC, LANES), F32),
        ),
        in_specs=[pl.BlockSpec(memory_space=pltpu.SMEM)] + vmem(4),
        out_specs=tuple(vmem(2)),
        scratch_shapes=[
            pltpu.VMEM((3 * REQ, 3 * LANES), BF16),
            pltpu.VMEM((ND * ROWS, LANES), F32),
            pltpu.VMEM((ND * ROWS, LANES), F32),
            pltpu.VMEM((3 * LOC * TL, 6 * LANES), BF16),
            pltpu.VMEM((6 * 32, 3 * LANES), BF16),
            pltpu.VMEM((8 * 32, 3 * LANES), BF16),
            pltpu.VMEM((NS, 8, LANES), F32),
            pltpu.VMEM((32, 8, LANES), F32),
            pltpu.VMEM((NG, 8, 8, LANES), F32),
            pltpu.VMEM((LOC, 2 * ITEMS), BF16),
            pltpu.VMEM((64, 2 * ITEMS), BF16),
            pltpu.VMEM((LANES, 2 * ITEMS), BF16),
            pltpu.VMEM((len(PAIRS) * LOC, 2 * ITEMS), BF16),
            dma((ND,)),
            dma((ND,)),
            dma((NS,)),
            dma((32,)),
            dma((UNITS,)),
            dma((UNITS,)),
            dma((NG,)),
            dma((NG,)),
        ],
        compiler_params=pltpu.CompilerParams(collective_id=0, has_side_effects=True),
        name="step",
    )(point_count, corr_scan, corr_tile, corr_src, samples.transpose(0, 2, 1, 3))
    hessian, gradient = pl.pallas_call(
        finish_kernel,
        out_shape=(
            jax.ShapeDtypeStruct((6, 6, LOC, LANES), F32),
            jax.ShapeDtypeStruct((4, 6), F32),
        ),
        in_specs=vmem(2),
        out_specs=tuple(vmem(2)),
        name="finish",
    )(block, parts)
    return hessian.transpose(2, 0, 1, 3), gradient


def solution(mesh):
    placed = (
        P("scan", "grp", None, None),
        P("scan"),
        P("scan", "grp"),
        P("scan", "grp"),
        P("scan", "grp", None),
    )
    return jax.shard_map(
        local,
        mesh=mesh,
        in_specs=placed,
        out_specs=(P("scan", None, None, "grp"), P(("scan", "grp"), None)),
        check_vma=False,
    )
```

time: 225 us -> 54.7 us (0.24)
  matrix products: 98.8 us -> 0 us
  Pallas kernels: 0 us -> 53.9 us
  starting transfers between devices: 44.5 us -> 0 us
  local copies, waits for them, and re-layouts: 36.7 us -> 0 us
  waiting for transfers between devices: 27.3 us -> 0 us
  other arithmetic: 14.7 us -> 0 us
    dot_general x20 -> x0, matrix products: 98.8 us -> none  [the longest x16 83.2 us: one_block(): jnp.dot(position, selector, precision=lax.Precision.HIGHEST, preferred_el...]
    pallas_call x0 -> x2, Pallas kernels: none -> 53.9 us  [the longest x1 52.2 us: local(): pl.pallas_call(step_kernel, out_shape=(jax.ShapeDtypeStruct((len(PAIRS) *...]
    all_to_all x6 -> x0, starting transfers between devices: 44.5 us -> none  [the longest x1 11.5 us: local(): lax.all_to_all(request_ids, ('scan', 'grp'), split_axis=0, concat_axis=0,...]
    all_to_all x6 -> x0, waiting for transfers between devices: 27.3 us -> none  [the longest x2 14.8 us: summed_on_arrival(): blocks = lax.all_to_all(cut_along(x, dim, length), axis, 0, 0, tiled=True)]
    gather x3 -> x0, other arithmetic: 10.1 us -> none  [the longest x1 10.1 us: masked_tiles(): limits = point_count[scan_local]]
    scatter x2 -> x0, local copies, waits for them, and re-layouts: 8.19 us -> none  [the longest x1 6.97 us: local(): sent_points = jnp.zeros((device_count * slot_cap, 4, 128), jnp.float32).a...]
    reshape x10 -> x0, local copies, waits for them, and re-layouts: 8.16 us -> none  [the longest x3 2.41 us: local(): target_scan = corr_scan.reshape(-1)]
    gather x7 -> x0, local copies, waits for them, and re-layouts: 4.33 us -> none  [the longest x1 1.88 us: masked_tiles(): picked = tile_table[safe_codes]]
  transfers between devices with their start and end apart: 6 -> 0, of which waited for: 4 -> 0; matrix products, arithmetic and copies ran while one was open for 60% -> 0% of each run, Pallas kernels for 0% -> 0%
where the time goes in v2:
time: 54.7 us; the launch traced here: 54.6 us
  Pallas kernels  53.9 us (99%)
  between operations  0.64 us (1%)
    pallas_call x1, Pallas kernels, local(): pl.pallas_call(step_kernel, out_shape=(jax.ShapeDtypeStruct((len(PAIRS) *...  52.2 us
    pallas_call x1, Pallas kernels, local(): pl.pallas_call(finish_kernel, out_shape=(jax.ShapeDtypeStruct((6, 6, LOC,...  1.78 us

profile of v2, /device:TPU:1, one launch (start us, length us, event | category | flops | bytes accessed | tf_op | source)
XLA Modules:
  0.0 54.6 jit_solution(11102214855740884083)
XLA Ops:
  0.6 52.2 %step.1 = (f32[336,128]{1,0:T(8,128)}, f32[4,16,128]{2,1,0:T(8,128)}) custom-call(s32[16]{0:T(128)} %pc_ref.1, s32[16,16]{1,0:T(8,128)} %cs_ref.1, s32[16,16]{1,0:T(8,128)} %ct_ref.1, s32[16,16,128]{2,1,0:T(8,128)} %src_ref.1, f32[16,6,16,128]{3,2,1,0:T(8,128)} %bitcast.2), custom_call_target="tpu_custom_call" | custom-call | tf_op jit(solution)/shard_map/step/pallas_call | solution.py:437
  52.8 1.8 %finish.1 = (f32[6,6,16,128]{3,2,1,0:T(8,128)}, f32[4,6]{1,0:T(4,128)}) custom-call(f32[336,128]{1,0:T(8,128)} %get-tuple-element.6.block_ref, f32[4,16,128]{2,1,0:T(8,128)} %get-tuple-element.7.part_ref), custom_call_target="tpu_custom_call" | custom-call | tf_op jit(solution)/shard_map/finish/pallas_call | solution.py:471

commit v3 on v2

--- a/solution.py
+++ b/solution.py
@@ -236,8 +236,16 @@
     block_ref[...] = dot_t(lhs_ref[...], column_ref[...])
 
 
+def low(x, bits):
+    return lax.bitwise_and(x, (1 << bits) - 1)
+
+
+def high(x, bits):
+    return lax.shift_right_logical(x, bits)
+
+
 def order(p):
-    return 2 * (1 - p % 2) + (p % 2 + p // 2) % 2
+    return 2 * (1 - low(p, 1)) + low(p + high(p, 1), 1)
 
 
 def step_kernel(
@@ -248,14 +256,14 @@
 ):
     row = lax.axis_index("scan")
     col = lax.axis_index("grp")
-    z, y, core = row // 8, (row // 2) % 4, row % 2
+    z, y, core = high(row, 3), low(high(row, 1), 2), low(row, 1)
     me = row * NG + col
     barrier = pltpu.get_barrier_semaphore()
 
     @pl.loop(1, ND)
     def _(step):
-        other = (me + step) % ND
-        pl.semaphore_signal(barrier, inc=1, device_id=(other // NG, other % NG), device_id_type=MESH)
+        other = low(me + step, 7)
+        pl.semaphore_signal(barrier, inc=1, device_id=(high(other, 2), low(other, 2)), device_id_type=MESH)
 
     pick_points(pc_ref, src_ref, sm_ref, pay_ref, col)
     pack(cs_ref, ct_ref, pay_ref, msg_ref, col)
@@ -273,11 +281,11 @@
         )
 
     def each_of_unit(u, sign, act):
-        uz = (z + sign * order(u // 4) + 4) % 4
-        uy = (y + sign * order(u % 4) + 4) % 4
+        uz = low(z + sign * order(high(u, 2)) + 4, 2)
+        uy = low(y + sign * order(low(u, 2)) + 4, 2)
         for dc in range(2):
             for dx in range(NG):
-                there = ((uz * 4 + uy) * 2 + (core + dc) % 2, (col + dx) % NG)
+                there = ((uz * 4 + uy) * 2 + low(core + dc, 1), low(col + dx, 2))
                 if dc == 0 and dx == 0:
 
                     @pl.when(u < UNITS - 1)
@@ -299,8 +307,8 @@
 
     tile_table(pc_ref, sm_ref, table_ref, col)
 
-    home = row // 8
-    slot = (row % 8) * NG + col
+    home = high(row, 3)
+    slot = low(row, 3) * NG + col
 
     def give(to_row, at):
         return pltpu.make_async_remote_copy(
@@ -318,7 +326,7 @@
             dst_ref=in_ref.at[from_col, pl.ds(2 * at, 2)],
             send_sem=send_b.at[unit],
             recv_sem=recv_b.at[from_col * 4 + at],
-            device_id=(row, unit // 4),
+            device_id=(row, high(unit, 2)),
             device_id_type=MESH,
         )
 
@@ -345,14 +353,14 @@
             def _():
                 pltpu.make_async_copy(back_ref.at[to_row], out_ref.at[slot], recv_a.at[slot]).start()
 
-        @pl.when(unit // 4 != col)
+        @pl.when(high(unit, 2) != col)
         def _():
-            share(unit, col, unit % 4).start()
-
-        @pl.when(unit // 4 == col)
+            share(unit, col, low(unit, 2)).start()
+
+        @pl.when(high(unit, 2) == col)
         def _():
             pltpu.make_async_copy(
-                back_ref.at[pl.ds(2 * unit, 2)], in_ref.at[col, pl.ds(2 * (unit % 4), 2)], recv_b.at[col * 4 + unit % 4]
+                back_ref.at[pl.ds(2 * unit, 2)], in_ref.at[col, pl.ds(2 * low(unit, 2), 2)], recv_b.at[col * 4 + low(unit, 2)]
             ).start()
 
     @pl.loop(0, 32)
@@ -361,7 +369,7 @@
 
     @pl.loop(0, UNITS)
     def _(n):
-        share(0, n // 4, n % 4).wait_recv()
+        share(0, high(n, 2), low(n, 2)).wait_recv()
 
     def load(q, m):
         return out_ref[q * 8 + m] if q < GROUPS // 2 else in_ref[q - GROUPS // 2, m]
@@ -381,14 +389,14 @@
         )
 
     for step in range(1, NG):
-        spread((col + step) % NG, col).start()
+        spread(low(col + step, 2), col).start()
 
     matrix(owner_ref, sums_ref, column_ref, lhs_ref, block_ref)
 
     @pl.loop(1, ND)
     def _(step):
-        other = (me + step) % ND
-        points(other // NG, other % NG, me).wait_send()
+        other = low(me + step, 7)
+        points(high(other, 2), low(other, 2), me).wait_send()
 
     @pl.loop(0, NS)
     def _(n):
@@ -398,12 +406,12 @@
 
     @pl.loop(0, UNITS)
     def _(n):
-        @pl.when(n // 4 != col)
+        @pl.when(high(n, 2) != col)
         def _():
-            share(n, col, n % 4).wait_send()
+            share(n, col, low(n, 2)).wait_send()
 
     for step in range(1, NG):
-        other = (col + step) % NG
+        other = low(col + step, 2)
         spread(other, col).wait_send()
         spread(other, other).wait_recv()
 

time: 54.7 us -> 51.7 us (0.945)
  Pallas kernels: 53.9 us -> 50.9 us
    pallas_call x1, Pallas kernels: 52.2 us -> 49.1 us  [local(): pl.pallas_call(step_kernel, out_shape=(jax.ShapeDtypeStruct((len(PAIRS) *...]
where the time goes in v3:
time: 51.7 us; the launch traced here: 51.5 us
  Pallas kernels  50.9 us (98%)
  between operations  0.64 us (1%)
    pallas_call x1, Pallas kernels, local(): pl.pallas_call(step_kernel, out_shape=(jax.ShapeDtypeStruct((len(PAIRS) *...  49.1 us
    pallas_call x1, Pallas kernels, local(): pl.pallas_call(finish_kernel, out_shape=(jax.ShapeDtypeStruct((6, 6, LOC,...  1.78 us

profile of v3, /device:TPU:1, one launch (start us, length us, event | category | flops | bytes accessed | tf_op | source)
XLA Modules:
  0.0 51.5 jit_solution(15546648539872593985)
XLA Ops:
  0.6 49.1 %step.1 = (f32[336,128]{1,0:T(8,128)}, f32[4,16,128]{2,1,0:T(8,128)}) custom-call(s32[16]{0:T(128)} %pc_ref.1, s32[16,16]{1,0:T(8,128)} %cs_ref.1, s32[16,16]{1,0:T(8,128)} %ct_ref.1, s32[16,16,128]{2,1,0:T(8,128)} %src_ref.1, f32[16,6,16,128]{3,2,1,0:T(8,128)} %bitcast.2), custom_call_target="tpu_custom_call" | custom-call | tf_op jit(solution)/shard_map/step/pallas_call | solution.py:445
  49.7 1.8 %finish.1 = (f32[6,6,16,128]{3,2,1,0:T(8,128)}, f32[4,6]{1,0:T(4,128)}) custom-call(f32[336,128]{1,0:T(8,128)} %get-tuple-element.6.block_ref, f32[4,16,128]{2,1,0:T(8,128)} %get-tuple-element.7.part_ref), custom_call_target="tpu_custom_call" | custom-call | tf_op jit(solution)/shard_map/finish/pallas_call | solution.py:479

commit v4 on v3

v4 whole, which is shorter than its diff:
```python
import functools

import jax
import jax.numpy as jnp
from jax import lax
from jax.experimental import pallas as pl
from jax.experimental.pallas import tpu as pltpu
from jax.sharding import PartitionSpec as P

F32 = jnp.float32
BF16 = jnp.bfloat16
I32 = jnp.int32
MESH = pl.DeviceIdType.MESH

NS = 32
NG = 4
ND = NS * NG
LOC = 16
TL = 16
CT = 16
REQ = LOC * CT
CAP = 4
FAR = 1000.0
LANES = 128
PAIRS = [(i, j) for i in range(6) for j in range(i, 6)]
PLANES = 4
SLOTS = ND * CAP
HALF = PLANES * LANES
SPOT = {(i, j): (i, j) for i in range(4) for j in range(i, 7)}
SPOT |= {(5, 5): (1, 0), (5, 6): (1, 7), (4, 4): (2, 1), (4, 5): (2, 0), (4, 6): (2, 7)}


def iota(shape, dim):
    return lax.broadcasted_iota(I32, shape, dim)


def dot(a, b):
    return lax.dot_general(a, b, (((1,), (0,)), ((), ())), preferred_element_type=F32)


def dot_t(a, b):
    return lax.dot_general(a, b, (((1,), (1,)), ((), ())), preferred_element_type=F32)


def parts_of(x, count):
    terms = []
    for _ in range(count):
        term = x.astype(BF16)
        terms.append(term)
        x = x - term.astype(F32)
    return terms


def onehot(cond):
    return jnp.where(cond, 1.0, 0.0).astype(BF16)


def low(x, bits):
    return lax.bitwise_and(x, (1 << bits) - 1)


def high(x, bits):
    return lax.shift_right_logical(x, bits)


def pick_points(x, pc_ref, src_ref, sm_ref, pay_ref, group):
    first = group * (TL * LANES)

    @pl.loop(0, LOC)
    def _(s):
        picks = src_ref[s]
        tile = high(picks, 7)
        lane = low(picks, 7)
        acc = jnp.zeros((CT, LANES), F32)
        for t in range(TL):
            row = jnp.broadcast_to(sm_ref[s, x, pl.ds(t, 1), :], (CT, LANES))
            got = jnp.take_along_axis(row, lane, axis=1, mode="promise_in_bounds")
            acc = jnp.where(tile == t, got, acc)
        if x == 0:
            acc = jnp.where(first + picks < pc_ref[s], acc, FAR)
        at = pl.multiple_of(s * CT, CT)
        for n, term in enumerate(parts_of(acc, 3)):
            pay_ref[pl.ds(n * REQ + at, CT), :] = term


def route(cs_ref, ct_ref, take_ref, code_ref, group):
    cs = cs_ref[...]
    ct = ct_ref[...]
    dest = (high(cs, 4) * NG + high(ct, 4)).astype(F32)
    code = (low(cs, 4) * TL + low(ct, 4) + 1).astype(F32)
    wide = dot(dest.astype(BF16), onehot(iota((CT, REQ), 1) % CT == iota((CT, REQ), 0)))
    wide = jnp.where(iota((LOC, REQ), 1) // CT == iota((LOC, REQ), 0), wide, 0.0)
    dest_t = dot(jnp.ones((ND, LOC), BF16), wide.astype(BF16))
    to_me = dest_t == iota((ND, REQ), 0).astype(F32)
    rank = dot(onehot(to_me), onehot(iota((REQ, REQ), 0) < iota((REQ, REQ), 1)))
    takes = [onehot(to_me & (rank == float(r))) for r in range(CAP)]
    for r in range(CAP):
        for n in range(3):
            take_ref[r * ND : (r + 1) * ND, n * REQ : (n + 1) * REQ] = takes[r]
    tall = dot(onehot(iota((REQ, LOC), 0) // CT == iota((REQ, LOC), 1)), code.astype(BF16))
    tall = jnp.where(iota((REQ, CT), 0) % CT == iota((REQ, CT), 1), tall, 0.0)
    code_b = dot(tall.astype(BF16), jnp.ones((CT, LANES), BF16))
    target = high(code_b.astype(I32) - 1, 4).astype(F32)
    source = (iota((REQ, LANES), 0) // CT).astype(F32)
    lane = iota((REQ, LANES), 1)
    codes = jnp.where(lane < 16, source, jnp.where(lane < 32, target, code_b)).astype(BF16)
    lane = iota((ND, LANES), 1)
    row = jnp.zeros((ND, LANES), F32)
    for r in range(CAP):
        at = group * CAP + r
        here = (lane == at) | (lane == 16 + at) | (lane == 32 + r)
        row = jnp.where(here, dot(takes[r], codes), row)
    code_ref[...] = row


def pack(x, take_ref, pay_ref, msg_ref):
    got = dot(take_ref[...], pay_ref[...])
    for r in range(CAP):
        msg_ref[x, pl.ds(r, ND, stride=CAP), :] = got[r * ND : (r + 1) * ND]


def tile_table(pc_ref, sm_ref, table_ref, group):
    point = (group * TL + iota((TL, LANES), 0)) * LANES + iota((TL, LANES), 1)

    @pl.loop(0, LOC)
    def _(s):
        valid = point < pc_ref[s]
        at = pl.multiple_of(s * TL, TL)
        for x in range(6):
            value = sm_ref[s, x]
            if x >= 3:
                value = jnp.where(valid, value, 0.0)
            for n, term in enumerate(parts_of(value, 3)):
                table_ref[pl.ds(n * LOC * TL + at, TL), x * LANES : (x + 1) * LANES] = term


def fetch_tiles(code_ref, table_ref, tile_ref, note_ref):
    codes = code_ref[...].astype(BF16)
    spread = dot(onehot(iota((SLOTS, ND), 0) // CAP == iota((SLOTS, ND), 1)), codes)
    spread = jnp.where(iota((SLOTS, LANES), 1) == 32 + iota((SLOTS, LANES), 0) % CAP, spread, 0.0)
    wanted = dot(spread.astype(BF16), jnp.ones((LANES, LOC * TL), BF16))
    take = onehot(wanted == (iota((SLOTS, LOC * TL), 1) + 1).astype(F32))
    tile_ref[...] = dot(jnp.concatenate([take] * 3, axis=1), table_ref[...])
    here = iota((ND, ND), 0)
    note_ref[...] = dot(onehot((here // 4 == iota((ND, ND), 1) // 4) & (here % 4 == 3)), codes)


def fold(a, b, clear, shift):
    return jnp.where(clear, a, b) + pltpu.roll(jnp.where(clear, b, a), shift, 0)


def plane_sums(plane, recv_ref, tile_ref, note_ref, left_ref, right_ref, back_ref):
    at = pl.multiple_of(plane * LANES, LANES)
    p = [recv_ref[x, pl.ds(at, LANES), :] for x in range(3)]
    tile = [tile_ref[pl.ds(at, LANES), x * LANES : (x + 1) * LANES] for x in range(6)]
    q, n = tile[:3], tile[3:]
    counts = p[0] < 0.5 * FAR
    p[0] = jnp.where(counts, p[0], 0.0)
    res = n[0] * (p[0] - q[0]) + n[1] * (p[1] - q[1]) + n[2] * (p[2] - q[2])
    w = jnp.where(counts, 1.0 / (1.0 + res * res), 0.0)
    jac = [
        p[1] * n[2] - p[2] * n[1],
        p[2] * n[0] - p[0] * n[2],
        p[0] * n[1] - p[1] * n[0],
        n[0],
        n[1],
        n[2],
    ]
    for i in range(6):
        big, small = parts_of(w * jac[i], 2)
        for r in range(8):
            for k, term in enumerate((big, big, small)):
                left_ref[r, i * 16 : (i + 1) * 16, k * LANES : (k + 1) * LANES] = term[r * 16 : (r + 1) * 16]
    for j, value in enumerate(jac + [res]):
        big, small = parts_of(value, 2)
        spots = [j] + {4: [9], 5: [8], 6: [15]}.get(j, [])
        for r in range(8):
            for k, term in enumerate((big, small, big)):
                for spot in spots:
                    right_ref[r, spot * 16 : (spot + 1) * 16, k * LANES : (k + 1) * LANES] = term[r * 16 : (r + 1) * 16]
    lane = iota((8, LANES), 1)
    sub = iota((8, LANES), 0)
    spot = lane // 16
    first = [spot < 8, (spot >= 1) & (spot <= 6), (spot >= 2) & (spot <= 6), spot < 8]
    other = [None, 5, 4, None]
    for chip in range(4):
        arrays = []
        for c in range(2):
            r = chip * 2 + c
            every = dot_t(left_ref[r], right_ref[r])
            for i in range(4):
                kept = jnp.zeros((8, LANES), F32)
                for h in range(2):
                    value = every[i * 16 + h * 8 : i * 16 + h * 8 + 8, :LANES]
                    if other[i] is not None:
                        o = other[i] * 16 + h * 8
                        value = jnp.where(first[i], value, every[o : o + 8, LANES:])
                    kept = jnp.where(lane % 16 == h * 8 + sub, value, kept)
                arrays.append(kept)
        for level in range(3):
            clear = (sub // (1 << level)) % 2 == 0
            arrays = [fold(arrays[n], arrays[n + 1], clear, 1 << level) for n in range(0, len(arrays), 2)]
        note = note_ref[pl.ds(plane * 32 + chip * 8, 8), :]
        back_ref[plane * 4 + chip] = jnp.where((sub % 4 == 3) & (spot < 3), note, arrays[0])


def turn(plane, mid_ref, back_ref, turn_ref):
    lane = iota((8, LANES), 1)
    blocks = [mid_ref[plane * 4 + m] for m in range(4)] + [back_ref[plane * 4 + m] for m in range(4)]
    for bit in range(3):
        shift = 16 << bit
        clear = (lane // shift) % 2 == 0
        for m in range(8):
            if (m >> bit) % 2 == 0:
                a, b = blocks[m], blocks[m + (1 << bit)]
                blocks[m] = jnp.where(clear, a, pltpu.roll(b, shift, 1))
                blocks[m + (1 << bit)] = jnp.where(clear, pltpu.roll(a, LANES - shift, 1), b)
    for n in range(8):
        turn_ref[plane, n] = jnp.where(lane < 64, blocks[n], -blocks[n]) if n >= 6 else blocks[n]


def arrange(turn_ref, owner_ref, sums_ref, column_ref):
    lane = iota((1, LANES), 1)
    y = (lane // 16) % 4
    for t in range(PLANES):
        source = turn_ref[t, 0]
        target = turn_ref[t, 1]
        for c in range(2):
            s = source[c * 4 + 3 : c * 4 + 4, :]
            b = target[c * 4 + 3 : c * 4 + 4, :]
            owner = jnp.broadcast_to(jnp.where(lane < 64, s, b), (LOC, LANES))
            at = c * HALF + t * LANES
            owner_ref[:, at : at + LANES] = onehot(owner == iota((LOC, LANES), 0).astype(F32))
            if column_ref is not None:
                column = jnp.where(lane < 64, b, s) + (16 * (2 * y + c)).astype(F32)
                there = jnp.broadcast_to(column, (LANES, LANES)) == iota((LANES, LANES), 0).astype(F32)
                there = jnp.where(there, -1.0, 0.0).astype(BF16)
                for n in range(2):
                    column_ref[:, n * 2 * HALF + at : n * 2 * HALF + at + LANES] = there
        for p in range(0, 8, 2):
            pair = jnp.concatenate([turn_ref[t, p], turn_ref[t, p + 1]], axis=0)
            for n, term in enumerate(parts_of(pair, 2)):
                sums_ref[p * 8 : p * 8 + 16, n * HALF + t * LANES : n * HALF + (t + 1) * LANES] = term


def scan_sums(owner_ref, sums_ref):
    owners = [jnp.concatenate([owner_ref[:, c * HALF : (c + 1) * HALF]] * 2, axis=1) for c in range(2)]
    both = dot_t(jnp.concatenate(owners, axis=0), sums_ref[...])
    lane = iota((LOC, 64), 1)
    part = jnp.where((lane // 4) % 2 == 0, both[:LOC], both[LOC:])
    return jnp.concatenate([part, jnp.zeros((LOC, LANES - 64), F32)], axis=1)


def matrix(owner_ref, sums_ref, column_ref, lhs_ref, block_ref):
    for k, pair in enumerate(PAIRS):
        i, p = SPOT[pair]
        for c in range(2):
            at = p * 8 + c * 4 + i
            mine = owner_ref[:, c * HALF : (c + 1) * HALF]
            for n in range(2):
                row = sums_ref[at : at + 1, n * HALF : (n + 1) * HALF]
                lhs_ref[k * LOC : (k + 1) * LOC, (2 * n + c) * HALF : (2 * n + c + 1) * HALF] = (
                    jnp.broadcast_to(row, (LOC, HALF)) * mine
                )
    block_ref[...] = dot_t(lhs_ref[...], column_ref[...])


def order(p):
    return 2 * (1 - low(p, 1)) + low(p + high(p, 1), 1)


def step_kernel(
    pc_ref, cs_any, ct_any, src_any, sm_any, block_ref, part_ref,
    cs_ref, ct_ref, src_ref, sm_ref, take_ref, pay_ref, code_ref, msg_ref, codes_ref, recv_ref, table_ref, tile_ref, note_ref,
    left_ref, right_ref, back_ref, mid_ref, turn_ref, got_ref, owner_ref, sums_ref, column_ref, lhs_ref,
    load_sem, send_p, recv_n, recv_p, send_a, recv_a, send_b, recv_b, send_c, recv_c,
):
    row = lax.axis_index("scan")
    col = lax.axis_index("grp")
    z, y, core = high(row, 3), low(high(row, 1), 2), low(row, 1)
    me = row * NG + col
    barrier = pltpu.get_barrier_semaphore()

    @pl.loop(1, ND)
    def _(step):
        other = low(me + step, 7)
        pl.semaphore_signal(barrier, inc=1, device_id=(high(other, 2), low(other, 2)), device_id_type=MESH)

    loads = [
        pltpu.make_async_copy(a, b, load_sem.at[n])
        for n, (a, b) in enumerate(
            [(cs_any, cs_ref), (ct_any, ct_ref), (src_any, src_ref)]
            + [(sm_any.at[:, x], sm_ref.at[:, x]) for x in range(3)]
            + [(sm_any.at[:, pl.ds(3, 3)], sm_ref.at[:, pl.ds(3, 3)])]
        )
    ]
    for load in loads:
        load.start()

    def to_all(act):
        @pl.loop(0, 16)
        def _(u):
            uz = low(z + order(high(u, 2)), 2)
            uy = low(y + order(low(u, 2)), 2)
            for dc in range(2):
                for dx in range(NG):
                    there = ((uz * 4 + uy) * 2 + low(core + dc, 1), low(col + dx, 2))
                    if dc == 0 and dx == 0:

                        @pl.when(u < 15)
                        def _():
                            act(*there)

                    else:
                        act(*there)

    def send_codes(r, c):
        pltpu.make_async_remote_copy(
            src_ref=code_ref.at[pl.ds(r * NG + c, 1)],
            dst_ref=codes_ref.at[pl.ds(me, 1)],
            send_sem=send_p.at[3],
            recv_sem=recv_n,
            device_id=(r, c),
            device_id_type=MESH,
        ).start()

    def send_points(x, r, c):
        pltpu.make_async_remote_copy(
            src_ref=msg_ref.at[x, pl.ds((r * NG + c) * CAP, CAP)],
            dst_ref=recv_ref.at[x, pl.ds(me * CAP, CAP)],
            send_sem=send_p.at[x],
            recv_sem=recv_p.at[z],
            device_id=(r, c),
            device_id_type=MESH,
        ).start()

    loads[0].wait()
    loads[1].wait()
    route(cs_ref, ct_ref, take_ref, code_ref, col)
    loads[2].wait()
    for x in range(3):
        loads[3 + x].wait()
        pick_points(x, pc_ref, src_ref, sm_ref, pay_ref.at[x], col)
        pack(x, take_ref, pay_ref.at[x], msg_ref)
        if x == 0:
            pl.semaphore_wait(barrier, ND - 1)
            pltpu.make_async_copy(code_ref.at[pl.ds(me, 1)], codes_ref.at[pl.ds(me, 1)], recv_n).start()
            to_all(send_codes)
        to_all(functools.partial(send_points, x))
    pltpu.make_async_copy(
        msg_ref.at[:, pl.ds(me * CAP, CAP)], recv_ref.at[:, pl.ds(me * CAP, CAP)], recv_p.at[z]
    ).start()

    loads[6].wait()
    tile_table(pc_ref, sm_ref, table_ref, col)
    for spot in (7, 10, 11, 12, 13, 14):
        right_ref[:, spot * 16 : (spot + 1) * 16, :] = jnp.zeros((8, 16, 3 * LANES), BF16)
    pltpu.make_async_copy(codes_ref, codes_ref, recv_n).wait()
    fetch_tiles(codes_ref, table_ref, tile_ref, note_ref)

    @pl.loop(0, PLANES)
    def _(u):
        plane = low(z + order(u), 2)
        arrived = recv_ref.at[:, pl.ds(plane * LANES, LANES)]
        pltpu.make_async_copy(arrived, arrived, recv_p.at[plane]).wait()
        plane_sums(plane, recv_ref, tile_ref, note_ref, left_ref, right_ref, back_ref)
        for n in range(8):
            to_row = plane * 8 + n
            src = back_ref.at[plane * 4 + n // 2, pl.ds(n % 2 * 4, 4)]
            dst = mid_ref.at[high(row, 1), pl.ds(core * 4, 4)]

            @pl.when(to_row != row)
            def _():
                pltpu.make_async_remote_copy(
                    src_ref=src,
                    dst_ref=dst,
                    send_sem=send_a,
                    recv_sem=recv_a,
                    device_id=(to_row, col),
                    device_id_type=MESH,
                ).start()

            @pl.when(to_row == row)
            def _():
                pltpu.make_async_copy(src, dst, recv_a).start()

    pltpu.make_async_copy(mid_ref, mid_ref, recv_a).wait()

    def give(to_col, at):
        return pltpu.make_async_remote_copy(
            src_ref=turn_ref.at[to_col],
            dst_ref=got_ref.at[at],
            send_sem=send_b.at[to_col],
            recv_sem=recv_b.at[at],
            device_id=(row, to_col),
            device_id_type=MESH,
        )

    def spread(to_col, at):
        return pltpu.make_async_remote_copy(
            src_ref=part_ref.at[col],
            dst_ref=part_ref.at[at],
            send_sem=send_c.at[to_col],
            recv_sem=recv_c.at[at],
            device_id=(row, to_col),
            device_id_type=MESH,
        )

    for plane in range(PLANES):
        turn(plane, mid_ref, back_ref, turn_ref)
    for step in (2, 1, 3):
        give(low(col + step, 2), col).start()
    own = pltpu.make_async_copy(turn_ref.at[col], got_ref.at[col], recv_b.at[col])
    own.start()
    arrange(turn_ref, owner_ref, sums_ref, None)
    part_ref[col] = scan_sums(owner_ref, sums_ref)
    for step in (2, 1, 3):
        spread(low(col + step, 2), col).start()

    for x in range(3):
        left = msg_ref.at[x, pl.ds(0, (ND - 1) * CAP)]
        pltpu.make_async_copy(left, left, send_p.at[x]).wait()
    left = code_ref.at[pl.ds(0, ND - 1)]
    pltpu.make_async_copy(left, left, send_p.at[3]).wait()
    for left in (back_ref.at[pl.ds(0, 15)], back_ref.at[15, pl.ds(0, 4)]):
        pltpu.make_async_copy(left, left, send_a).wait()

    own.wait()
    for step in range(1, NG):
        other = low(col + step, 2)
        give(other, other).wait_recv()
    arrange(got_ref, owner_ref, sums_ref, column_ref)
    matrix(owner_ref, sums_ref, column_ref, lhs_ref, block_ref)
    for step in range(1, NG):
        other = low(col + step, 2)
        give(other, col).wait_send()
        spread(other, col).wait_send()
        spread(other, other).wait_recv()


def finish_kernel(block_ref, part_ref, hess_ref, grad_ref):
    row = lax.axis_index("scan")
    col = lax.axis_index("grp")
    total = part_ref[0] + part_ref[1] + part_ref[2] + part_ref[3]
    total = total + pltpu.roll(total, LANES - 4, 1)
    lane = iota((LOC, LANES), 1)
    diag = (lane == iota((LOC, LANES), 0) + LOC * (row % 8)) & (row // 8 == col)
    for k, (i, j) in enumerate(PAIRS):
        at = SPOT[i, j][1] * 8 + SPOT[i, j][0]
        value = block_ref[k * LOC : (k + 1) * LOC, :] + jnp.where(
            diag, jnp.broadcast_to(total[:, at : at + 1], (LOC, LANES)), 0.0
        )
        hess_ref[i, j] = value
        if i != j:
            hess_ref[j, i] = value
    some = jnp.zeros((4, LANES), F32)
    for n in range(NG):
        some = jnp.where(col == n, total[n * 4 : (n + 1) * 4, :], some)
    at = [SPOT[i, 6][1] * 8 + SPOT[i, 6][0] for i in range(6)]
    grad_ref[...] = jnp.concatenate([some[:, a : a + 1] for a in at], axis=1)


def vmem(count):
    return [pl.BlockSpec(memory_space=pltpu.VMEM)] * count


def local(samples, point_count, corr_scan, corr_tile, corr_src):
    dma = pltpu.SemaphoreType.DMA
    block, parts = pl.pallas_call(
        step_kernel,
        out_shape=(
            jax.ShapeDtypeStruct((len(PAIRS) * LOC, LANES), F32),
            jax.ShapeDtypeStruct((NG, LOC, LANES), F32),
        ),
        in_specs=[pl.BlockSpec(memory_space=pltpu.SMEM)] + [pl.BlockSpec(memory_space=pl.ANY)] * 4,
        out_specs=tuple(vmem(2)),
        scratch_shapes=[
            pltpu.VMEM((LOC, CT), I32),
            pltpu.VMEM((LOC, CT), I32),
            pltpu.VMEM((LOC, CT, LANES), I32),
            pltpu.VMEM((LOC, 6, TL, LANES), F32),
            pltpu.VMEM((SLOTS, 3 * REQ), BF16),
            pltpu.VMEM((3, 3 * REQ, LANES), BF16),
            pltpu.VMEM((ND, LANES), F32),
            pltpu.VMEM((3, SLOTS, LANES), F32),
            pltpu.VMEM((ND, LANES), F32),
            pltpu.VMEM((3, SLOTS, LANES), F32),
            pltpu.VMEM((3 * LOC * TL, 6 * LANES), BF16),
            pltpu.VMEM((SLOTS, 6 * LANES), F32),
            pltpu.VMEM((ND, LANES), F32),
            pltpu.VMEM((8, 6 * 16, 3 * LANES), BF16),
            pltpu.VMEM((8, 16 * 16, 3 * LANES), BF16),
            pltpu.VMEM((16, 8, LANES), F32),
            pltpu.VMEM((16, 8, LANES), F32),
            pltpu.VMEM((PLANES, 8, 8, LANES), F32),
            pltpu.VMEM((NG, 8, 8, LANES), F32),
            pltpu.VMEM((LOC, 2 * HALF), BF16),
            pltpu.VMEM((64, 2 * HALF), BF16),
            pltpu.VMEM((LANES, 4 * HALF), BF16),
            pltpu.VMEM((len(PAIRS) * LOC, 4 * HALF), BF16),
            dma((7,)),
            dma((4,)),
            dma,
            dma((PLANES,)),
            dma,
            dma,
            dma((NG,)),
            dma((NG,)),
            dma((NG,)),
            dma((NG,)),
        ],
        compiler_params=pltpu.CompilerParams(collective_id=0, has_side_effects=True),
        name="step",
    )(point_count, corr_scan, corr_tile, corr_src, samples.transpose(0, 2, 1, 3))
    hessian, gradient = pl.pallas_call(
        finish_kernel,
        out_shape=(
            jax.ShapeDtypeStruct((6, 6, LOC, LANES), F32),
            jax.ShapeDtypeStruct((4, 6), F32),
        ),
        in_specs=vmem(2),
        out_specs=tuple(vmem(2)),
        name="finish",
    )(block, parts)
    return hessian.transpose(2, 0, 1, 3), gradient


def solution(mesh):
    placed = (
        P("scan", "grp", None, None),
        P("scan"),
        P("scan", "grp"),
        P("scan", "grp"),
        P("scan", "grp", None),
    )
    return jax.shard_map(
        local,
        mesh=mesh,
        in_specs=placed,
        out_specs=(P("scan", None, None, "grp"), P(("scan", "grp"), None)),
        check_vma=False,
    )
```

time: 51.7 us -> 39.8 us (0.77)
  Pallas kernels: 50.9 us -> 39 us
    pallas_call x1, Pallas kernels: 49.1 us -> 37.1 us  [local(): pl.pallas_call(step_kernel, out_shape=(jax.ShapeDtypeStruct((len(PAIRS) *...]
where the time goes in v4:
time: 39.8 us; the launch traced here: 39.6 us
  Pallas kernels  39 us (98%)
  between operations  0.64 us (2%)
    pallas_call x1, Pallas kernels, local(): pl.pallas_call(step_kernel, out_shape=(jax.ShapeDtypeStruct((len(PAIRS) *...  37.1 us
    pallas_call x1, Pallas kernels, local(): pl.pallas_call(finish_kernel, out_shape=(jax.ShapeDtypeStruct((6, 6, LOC,...  1.85 us

profile of v4, /device:TPU:1, one launch (start us, length us, event | category | flops | bytes accessed | tf_op | source)
XLA Modules:
  0.0 39.6 jit_solution(9258563052338132561)
XLA Ops:
  0.6 37.1 %step.1 = (f32[336,128]{1,0:T(8,128)}, f32[4,16,128]{2,1,0:T(8,128)}) custom-call(s32[16]{0:T(128)} %pc_ref.1, s32[16,16]{1,0:T(8,128)} %cs_any.1, s32[16,16]{1,0:T(8,128)} %ct_any.1, s32[16,16,128]{2,1,0:T(8,128)} %src_any.1, f32[16,6,16,128]{3,2,1,0:T(8,128)} %bitcast.2), custom_call_target="tpu_custom_call" | custom-call | tf_op jit(solution)/shard_map/step/pallas_call | solution.py:469
  37.8 1.8 %finish.1 = (f32[6,6,16,128]{3,2,1,0:T(8,128)}, f32[4,6]{1,0:T(4,128)}) custom-call(f32[336,128]{1,0:T(8,128)} %get-tuple-element.6.block_ref, f32[4,16,128]{2,1,0:T(8,128)} %get-tuple-element.7.part_ref), custom_call_target="tpu_custom_call" | custom-call | tf_op jit(solution)/shard_map/finish/pallas_call | solution.py:515

commit v5 on v4

--- a/solution.py
+++ b/solution.py
@@ -25,6 +25,7 @@
 PAIRS = [(i, j) for i in range(6) for j in range(i, 6)]
 PLANES = 4
 SLOTS = ND * CAP
+FIRST = CAP + 1
 HALF = PLANES * LANES
 SPOT = {(i, j): (i, j) for i in range(4) for j in range(i, 7)}
 SPOT |= {(5, 5): (1, 0), (5, 6): (1, 7), (4, 4): (2, 1), (4, 5): (2, 0), (4, 6): (2, 7)}
@@ -83,7 +84,7 @@
             pay_ref[pl.ds(n * REQ + at, CT), :] = term
 
 
-def route(cs_ref, ct_ref, take_ref, code_ref, group):
+def route(cs_ref, ct_ref, take_ref, first_ref, group):
     cs = cs_ref[...]
     ct = ct_ref[...]
     dest = (high(cs, 4) * NG + high(ct, 4)).astype(F32)
@@ -110,13 +111,13 @@
         at = group * CAP + r
         here = (lane == at) | (lane == 16 + at) | (lane == 32 + r)
         row = jnp.where(here, dot(takes[r], codes), row)
-    code_ref[...] = row
-
-
-def pack(x, take_ref, pay_ref, msg_ref):
+    first_ref[pl.ds(CAP, ND, stride=FIRST), :] = row
+
+
+def pack(take_ref, pay_ref, msg_ref, rows):
     got = dot(take_ref[...], pay_ref[...])
     for r in range(CAP):
-        msg_ref[x, pl.ds(r, ND, stride=CAP), :] = got[r * ND : (r + 1) * ND]
+        msg_ref[pl.ds(r, ND, stride=rows), :] = got[r * ND : (r + 1) * ND]
 
 
 def tile_table(pc_ref, sm_ref, table_ref, group):
@@ -134,25 +135,29 @@
                 table_ref[pl.ds(n * LOC * TL + at, TL), x * LANES : (x + 1) * LANES] = term
 
 
-def fetch_tiles(code_ref, table_ref, tile_ref, note_ref):
-    codes = code_ref[...].astype(BF16)
-    spread = dot(onehot(iota((SLOTS, ND), 0) // CAP == iota((SLOTS, ND), 1)), codes)
-    spread = jnp.where(iota((SLOTS, LANES), 1) == 32 + iota((SLOTS, LANES), 0) % CAP, spread, 0.0)
+def fetch_tiles(first_ref, plane, table_ref, tile_ref, note_ref, x_ref):
+    src = plane * (32 * FIRST)
+    at = pl.multiple_of(plane * LANES, LANES)
+    codes = first_ref[pl.ds(src + CAP, 32, stride=FIRST), :].astype(BF16)
+    for r in range(CAP):
+        x_ref[pl.ds(r, 32, stride=CAP), :] = first_ref[pl.ds(src + r, 32, stride=FIRST), :]
+    spread = dot(onehot(iota((LANES, 32), 0) // CAP == iota((LANES, 32), 1)), codes)
+    spread = jnp.where(iota((LANES, LANES), 1) == 32 + iota((LANES, LANES), 0) % CAP, spread, 0.0)
     wanted = dot(spread.astype(BF16), jnp.ones((LANES, LOC * TL), BF16))
-    take = onehot(wanted == (iota((SLOTS, LOC * TL), 1) + 1).astype(F32))
+    take = onehot(wanted == (iota((LANES, LOC * TL), 1) + 1).astype(F32))
     tile_ref[...] = dot(jnp.concatenate([take] * 3, axis=1), table_ref[...])
-    here = iota((ND, ND), 0)
-    note_ref[...] = dot(onehot((here // 4 == iota((ND, ND), 1) // 4) & (here % 4 == 3)), codes)
+    here = iota((32, 32), 0)
+    note_ref[...] = dot(onehot((here // 4 == iota((32, 32), 1) // 4) & (here % 4 == 3)), codes)
 
 
 def fold(a, b, clear, shift):
     return jnp.where(clear, a, b) + pltpu.roll(jnp.where(clear, b, a), shift, 0)
 
 
-def plane_sums(plane, recv_ref, tile_ref, note_ref, left_ref, right_ref, back_ref):
+def plane_sums(plane, x_ref, recv_ref, tile_ref, note_ref, left_ref, right_ref, back_ref):
     at = pl.multiple_of(plane * LANES, LANES)
-    p = [recv_ref[x, pl.ds(at, LANES), :] for x in range(3)]
-    tile = [tile_ref[pl.ds(at, LANES), x * LANES : (x + 1) * LANES] for x in range(6)]
+    p = [x_ref[...]] + [recv_ref[x, pl.ds(at, LANES), :] for x in range(2)]
+    tile = [tile_ref[:, x * LANES : (x + 1) * LANES] for x in range(6)]
     q, n = tile[:3], tile[3:]
     counts = p[0] < 0.5 * FAR
     p[0] = jnp.where(counts, p[0], 0.0)
@@ -200,13 +205,13 @@
         for level in range(3):
             clear = (sub // (1 << level)) % 2 == 0
             arrays = [fold(arrays[n], arrays[n + 1], clear, 1 << level) for n in range(0, len(arrays), 2)]
-        note = note_ref[pl.ds(plane * 32 + chip * 8, 8), :]
+        note = note_ref[chip * 8 : chip * 8 + 8, :]
         back_ref[plane * 4 + chip] = jnp.where((sub % 4 == 3) & (spot < 3), note, arrays[0])
 
 
-def turn(plane, mid_ref, back_ref, turn_ref):
+def turn(plane, partner_ref, source_ref, turn_ref):
     lane = iota((8, LANES), 1)
-    blocks = [mid_ref[plane * 4 + m] for m in range(4)] + [back_ref[plane * 4 + m] for m in range(4)]
+    blocks = [ref[plane * 4 + m] for ref in (partner_ref, source_ref) for m in range(4)]
     for bit in range(3):
         shift = 16 << bit
         clear = (lane // shift) % 2 == 0
@@ -271,21 +276,16 @@
 
 def step_kernel(
     pc_ref, cs_any, ct_any, src_any, sm_any, block_ref, part_ref,
-    cs_ref, ct_ref, src_ref, sm_ref, take_ref, pay_ref, code_ref, msg_ref, codes_ref, recv_ref, table_ref, tile_ref, note_ref,
-    left_ref, right_ref, back_ref, mid_ref, turn_ref, got_ref, owner_ref, sums_ref, column_ref, lhs_ref,
-    load_sem, send_p, recv_n, recv_p, send_a, recv_a, send_b, recv_b, send_c, recv_c,
+    cs_ref, ct_ref, src_ref, sm_ref, take_ref, pay_ref, first_ref, msg_ref, firsts_ref, recv_ref, table_ref, tile_ref, note_ref,
+    x_ref, left_ref, right_ref, back_ref, mid_ref, out_ref, in_ref, turn_ref, owner_ref, sums_ref, column_ref, lhs_ref,
+    load_sem, send_p, recv_f, recv_p, send_a, recv_a, send_b, recv_b, send_c, recv_c,
 ):
     row = lax.axis_index("scan")
     col = lax.axis_index("grp")
     z, y, core = high(row, 3), low(high(row, 1), 2), low(row, 1)
     me = row * NG + col
+    chip = high(row, 1)
     barrier = pltpu.get_barrier_semaphore()
-
-    @pl.loop(1, ND)
-    def _(step):
-        other = low(me + step, 7)
-        pl.semaphore_signal(barrier, inc=1, device_id=(high(other, 2), low(other, 2)), device_id_type=MESH)
-
     loads = [
         pltpu.make_async_copy(a, b, load_sem.at[n])
         for n, (a, b) in enumerate(
@@ -302,8 +302,8 @@
         def _(u):
             uz = low(z + order(high(u, 2)), 2)
             uy = low(y + order(low(u, 2)), 2)
-            for dc in range(2):
-                for dx in range(NG):
+            for dx in (2, 1, 3, 0):
+                for dc in (1, 0):
                     there = ((uz * 4 + uy) * 2 + low(core + dc, 1), low(col + dx, 2))
                     if dc == 0 and dx == 0:
 
@@ -314,39 +314,36 @@
                     else:
                         act(*there)
 
-    def send_codes(r, c):
+    to_all(lambda r, c: pl.semaphore_signal(barrier, inc=1, device_id=(r, c), device_id_type=MESH))
+
+    def send(src, dst, sem, recv, r, c, rows):
         pltpu.make_async_remote_copy(
-            src_ref=code_ref.at[pl.ds(r * NG + c, 1)],
-            dst_ref=codes_ref.at[pl.ds(me, 1)],
-            send_sem=send_p.at[3],
-            recv_sem=recv_n,
+            src_ref=src.at[pl.ds((r * NG + c) * rows, rows)],
+            dst_ref=dst.at[pl.ds(me * rows, rows)],
+            send_sem=sem,
+            recv_sem=recv.at[z],
             device_id=(r, c),
             device_id_type=MESH,
         ).start()
 
-    def send_points(x, r, c):
-        pltpu.make_async_remote_copy(
-            src_ref=msg_ref.at[x, pl.ds((r * NG + c) * CAP, CAP)],
-            dst_ref=recv_ref.at[x, pl.ds(me * CAP, CAP)],
-            send_sem=send_p.at[x],
-            recv_sem=recv_p.at[z],
-            device_id=(r, c),
-            device_id_type=MESH,
-        ).start()
-
     loads[0].wait()
     loads[1].wait()
-    route(cs_ref, ct_ref, take_ref, code_ref, col)
+    route(cs_ref, ct_ref, take_ref, first_ref, col)
     loads[2].wait()
     for x in range(3):
         loads[3 + x].wait()
         pick_points(x, pc_ref, src_ref, sm_ref, pay_ref.at[x], col)
-        pack(x, take_ref, pay_ref.at[x], msg_ref)
         if x == 0:
+            pack(take_ref, pay_ref.at[x], first_ref, FIRST)
             pl.semaphore_wait(barrier, ND - 1)
-            pltpu.make_async_copy(code_ref.at[pl.ds(me, 1)], codes_ref.at[pl.ds(me, 1)], recv_n).start()
-            to_all(send_codes)
-        to_all(functools.partial(send_points, x))
+            to_all(lambda r, c: send(first_ref, firsts_ref, send_p.at[0], recv_f, r, c, FIRST))
+        else:
+            msg, got = msg_ref.at[x - 1], recv_ref.at[x - 1]
+            pack(take_ref, pay_ref.at[x], msg, CAP)
+            to_all(lambda r, c: send(msg, got, send_p.at[x], recv_p, r, c, CAP))
+    pltpu.make_async_copy(
+        first_ref.at[pl.ds(me * FIRST, FIRST)], firsts_ref.at[pl.ds(me * FIRST, FIRST)], recv_f.at[z]
+    ).start()
     pltpu.make_async_copy(
         msg_ref.at[:, pl.ds(me * CAP, CAP)], recv_ref.at[:, pl.ds(me * CAP, CAP)], recv_p.at[z]
     ).start()
@@ -355,19 +352,36 @@
     tile_table(pc_ref, sm_ref, table_ref, col)
     for spot in (7, 10, 11, 12, 13, 14):
         right_ref[:, spot * 16 : (spot + 1) * 16, :] = jnp.zeros((8, 16, 3 * LANES), BF16)
-    pltpu.make_async_copy(codes_ref, codes_ref, recv_n).wait()
-    fetch_tiles(codes_ref, table_ref, tile_ref, note_ref)
+
+    def cross(ref, plane, got, kind, at):
+        return pltpu.make_async_remote_copy(
+            src_ref=ref.at[pl.ds(plane * 4, 4)],
+            dst_ref=got.at[pl.ds(at * 4, 4)],
+            send_sem=send_b.at[kind, plane],
+            recv_sem=recv_b.at[kind, at],
+            device_id=(row, plane),
+            device_id_type=MESH,
+        )
+
+    def keep(ref, got, kind):
+        return pltpu.make_async_copy(
+            ref.at[pl.ds(col * 4, 4)], got.at[pl.ds(col * 4, 4)], recv_b.at[kind, col]
+        )
 
     @pl.loop(0, PLANES)
     def _(u):
         plane = low(z + order(u), 2)
+        arrived = firsts_ref.at[pl.ds(plane * (32 * FIRST), 32 * FIRST)]
+        pltpu.make_async_copy(arrived, arrived, recv_f.at[plane]).wait()
+        fetch_tiles(firsts_ref, plane, table_ref, tile_ref, note_ref, x_ref)
         arrived = recv_ref.at[:, pl.ds(plane * LANES, LANES)]
         pltpu.make_async_copy(arrived, arrived, recv_p.at[plane]).wait()
-        plane_sums(plane, recv_ref, tile_ref, note_ref, left_ref, right_ref, back_ref)
-        for n in range(8):
-            to_row = plane * 8 + n
-            src = back_ref.at[plane * 4 + n // 2, pl.ds(n % 2 * 4, 4)]
-            dst = mid_ref.at[high(row, 1), pl.ds(core * 4, 4)]
+        plane_sums(plane, x_ref, recv_ref, tile_ref, note_ref, left_ref, right_ref, back_ref)
+        for n in (4, 5, 2, 3, 6, 7, 0, 1):
+            to_chip = plane * 4 + low(y + n // 2, 2)
+            to_row = to_chip * 2 + n % 2
+            src = back_ref.at[to_chip, pl.ds(n % 2 * 4, 4)]
+            dst = mid_ref.at[chip, pl.ds(core * 4, 4)]
 
             @pl.when(to_row != row)
             def _():
@@ -375,26 +389,36 @@
                     src_ref=src,
                     dst_ref=dst,
                     send_sem=send_a,
-                    recv_sem=recv_a,
+                    recv_sem=recv_a.at[z],
                     device_id=(to_row, col),
                     device_id_type=MESH,
                 ).start()
 
             @pl.when(to_row == row)
             def _():
-                pltpu.make_async_copy(src, dst, recv_a).start()
-
-    pltpu.make_async_copy(mid_ref, mid_ref, recv_a).wait()
-
-    def give(to_col, at):
-        return pltpu.make_async_remote_copy(
-            src_ref=turn_ref.at[to_col],
-            dst_ref=got_ref.at[at],
-            send_sem=send_b.at[to_col],
-            recv_sem=recv_b.at[at],
-            device_id=(row, to_col),
-            device_id_type=MESH,
-        )
+                pltpu.make_async_copy(src, dst, recv_a.at[z]).start()
+
+        @pl.when(plane != col)
+        def _():
+            cross(back_ref, plane, in_ref, 0, col).start()
+
+        @pl.when(plane == col)
+        def _():
+            keep(back_ref, in_ref, 0).start()
+
+    @pl.loop(0, PLANES)
+    def _(u):
+        plane = low(z - order(u) + 4, 2)
+        arrived = mid_ref.at[pl.ds(plane * 4, 4)]
+        pltpu.make_async_copy(arrived, arrived, recv_a.at[plane]).wait()
+
+        @pl.when(plane != col)
+        def _():
+            cross(mid_ref, plane, out_ref, 1, col).start()
+
+        @pl.when(plane == col)
+        def _():
+            keep(mid_ref, out_ref, 1).start()
 
     def spread(to_col, at):
         return pltpu.make_async_remote_copy(
@@ -408,32 +432,31 @@
 
     for plane in range(PLANES):
         turn(plane, mid_ref, back_ref, turn_ref)
-    for step in (2, 1, 3):
-        give(low(col + step, 2), col).start()
-    own = pltpu.make_async_copy(turn_ref.at[col], got_ref.at[col], recv_b.at[col])
-    own.start()
     arrange(turn_ref, owner_ref, sums_ref, None)
     part_ref[col] = scan_sums(owner_ref, sums_ref)
     for step in (2, 1, 3):
         spread(low(col + step, 2), col).start()
 
-    for x in range(3):
+    left = first_ref.at[pl.ds(0, (ND - 1) * FIRST)]
+    pltpu.make_async_copy(left, left, send_p.at[0]).wait()
+    for x in range(2):
         left = msg_ref.at[x, pl.ds(0, (ND - 1) * CAP)]
-        pltpu.make_async_copy(left, left, send_p.at[x]).wait()
-    left = code_ref.at[pl.ds(0, ND - 1)]
-    pltpu.make_async_copy(left, left, send_p.at[3]).wait()
+        pltpu.make_async_copy(left, left, send_p.at[1 + x]).wait()
     for left in (back_ref.at[pl.ds(0, 15)], back_ref.at[15, pl.ds(0, 4)]):
         pltpu.make_async_copy(left, left, send_a).wait()
 
-    own.wait()
-    for step in range(1, NG):
-        other = low(col + step, 2)
-        give(other, other).wait_recv()
-    arrange(got_ref, owner_ref, sums_ref, column_ref)
+    for kind, got in enumerate((in_ref, out_ref)):
+        keep(got, got, kind).wait()
+        for step in range(1, NG):
+            cross(got, 0, got, kind, low(col + step, 2)).wait_recv()
+    for plane in range(PLANES):
+        turn(plane, out_ref, in_ref, turn_ref)
+    arrange(turn_ref, owner_ref, sums_ref, column_ref)
     matrix(owner_ref, sums_ref, column_ref, lhs_ref, block_ref)
     for step in range(1, NG):
         other = low(col + step, 2)
-        give(other, col).wait_send()
+        cross(back_ref, other, in_ref, 0, col).wait_send()
+        cross(mid_ref, other, out_ref, 1, col).wait_send()
         spread(other, col).wait_send()
         spread(other, other).wait_recv()
 
@@ -481,31 +504,33 @@
             pltpu.VMEM((LOC, 6, TL, LANES), F32),
             pltpu.VMEM((SLOTS, 3 * REQ), BF16),
             pltpu.VMEM((3, 3 * REQ, LANES), BF16),
-            pltpu.VMEM((ND, LANES), F32),
-            pltpu.VMEM((3, SLOTS, LANES), F32),
-            pltpu.VMEM((ND, LANES), F32),
-            pltpu.VMEM((3, SLOTS, LANES), F32),
+            pltpu.VMEM((ND * FIRST, LANES), F32),
+            pltpu.VMEM((2, SLOTS, LANES), F32),
+            pltpu.VMEM((ND * FIRST, LANES), F32),
+            pltpu.VMEM((2, SLOTS, LANES), F32),
             pltpu.VMEM((3 * LOC * TL, 6 * LANES), BF16),
-            pltpu.VMEM((SLOTS, 6 * LANES), F32),
-            pltpu.VMEM((ND, LANES), F32),
+            pltpu.VMEM((LANES, 6 * LANES), F32),
+            pltpu.VMEM((32, LANES), F32),
+            pltpu.VMEM((LANES, LANES), F32),
             pltpu.VMEM((8, 6 * 16, 3 * LANES), BF16),
             pltpu.VMEM((8, 16 * 16, 3 * LANES), BF16),
             pltpu.VMEM((16, 8, LANES), F32),
             pltpu.VMEM((16, 8, LANES), F32),
+            pltpu.VMEM((16, 8, LANES), F32),
+            pltpu.VMEM((16, 8, LANES), F32),
             pltpu.VMEM((PLANES, 8, 8, LANES), F32),
-            pltpu.VMEM((NG, 8, 8, LANES), F32),
             pltpu.VMEM((LOC, 2 * HALF), BF16),
             pltpu.VMEM((64, 2 * HALF), BF16),
             pltpu.VMEM((LANES, 4 * HALF), BF16),
             pltpu.VMEM((len(PAIRS) * LOC, 4 * HALF), BF16),
             dma((7,)),
-            dma((4,)),
+            dma((3,)),
+            dma((PLANES,)),
+            dma((PLANES,)),
             dma,
             dma((PLANES,)),
-            dma,
-            dma,
-            dma((NG,)),
-            dma((NG,)),
+            dma((2, NG)),
+            dma((2, NG)),
             dma((NG,)),
             dma((NG,)),
         ],

time: 39.8 us -> 39.2 us (0.985)
  Pallas kernels: 39 us -> 38.4 us
    pallas_call x1, Pallas kernels: 37.1 us -> 36.6 us  [local(): pl.pallas_call(step_kernel, out_shape=(jax.ShapeDtypeStruct((len(PAIRS) *...]
where the time goes in v5:
time: 39.2 us; the launch traced here: 39.1 us
  Pallas kernels  38.4 us (98%)
  between operations  0.64 us (2%)
    pallas_call x1, Pallas kernels, local(): pl.pallas_call(step_kernel, out_shape=(jax.ShapeDtypeStruct((len(PAIRS) *...  36.6 us
    pallas_call x1, Pallas kernels, local(): pl.pallas_call(finish_kernel, out_shape=(jax.ShapeDtypeStruct((6, 6, LOC,...  1.85 us

profile of v5, /device:TPU:1, one launch (start us, length us, event | category | flops | bytes accessed | tf_op | source)
XLA Modules:
  0.0 39.1 jit_solution(17303889405735477356)
XLA Ops:
  0.6 36.6 %step.1 = (f32[336,128]{1,0:T(8,128)}, f32[4,16,128]{2,1,0:T(8,128)}) custom-call(s32[16]{0:T(128)} %pc_ref.1, s32[16,16]{1,0:T(8,128)} %cs_any.1, s32[16,16]{1,0:T(8,128)} %ct_any.1, s32[16,16,128]{2,1,0:T(8,128)} %src_any.1, f32[16,6,16,128]{3,2,1,0:T(8,128)} %bitcast.2), custom_call_target="tpu_custom_call" | custom-call | tf_op jit(solution)/shard_map/step/pallas_call | solution.py:492
  37.2 1.8 %finish.1 = (f32[6,6,16,128]{3,2,1,0:T(8,128)}, f32[4,6]{1,0:T(4,128)}) custom-call(f32[336,128]{1,0:T(8,128)} %get-tuple-element.6.block_ref, f32[4,16,128]{2,1,0:T(8,128)} %get-tuple-element.7.part_ref), custom_call_target="tpu_custom_call" | custom-call | tf_op jit(solution)/shard_map/finish/pallas_call | solution.py:540

commit v6 on v4

--- a/solution.py
+++ b/solution.py
@@ -63,24 +63,28 @@
     return lax.shift_right_logical(x, bits)
 
 
-def pick_points(x, pc_ref, src_ref, sm_ref, pay_ref, group):
+def pick_points(pc_ref, src_ref, sm_ref, pay_ref, group):
     first = group * (TL * LANES)
-
-    @pl.loop(0, LOC)
-    def _(s):
+    for s in range(LOC):
         picks = src_ref[s]
-        tile = high(picks, 7)
-        lane = low(picks, 7)
-        acc = jnp.zeros((CT, LANES), F32)
-        for t in range(TL):
-            row = jnp.broadcast_to(sm_ref[s, x, pl.ds(t, 1), :], (CT, LANES))
-            got = jnp.take_along_axis(row, lane, axis=1, mode="promise_in_bounds")
-            acc = jnp.where(tile == t, got, acc)
-        if x == 0:
-            acc = jnp.where(first + picks < pc_ref[s], acc, FAR)
-        at = pl.multiple_of(s * CT, CT)
-        for n, term in enumerate(parts_of(acc, 3)):
-            pay_ref[pl.ds(n * REQ + at, CT), :] = term
+        halves = []
+        for h in range(2):
+            part = picks[h * 8 : h * 8 + 8]
+            tile = high(part, 7)
+            lane = low(part, 7)
+            acc = [jnp.zeros((8, LANES), F32) for _ in range(3)]
+            for t in range(TL):
+                here = tile == t
+                for x in range(3):
+                    row = jnp.broadcast_to(sm_ref[s, x, t : t + 1, :], (8, LANES))
+                    got = jnp.take_along_axis(row, lane, axis=1, mode="promise_in_bounds")
+                    acc[x] = jnp.where(here, got, acc[x])
+            acc[0] = jnp.where(first + part < pc_ref[s], acc[0], FAR)
+            halves.append(acc)
+        for x in range(3):
+            both = jnp.concatenate([halves[0][x], halves[1][x]], axis=0)
+            for n, term in enumerate(parts_of(both, 3)):
+                pay_ref[n * REQ + s * CT : n * REQ + (s + 1) * CT, x * LANES : (x + 1) * LANES] = term
 
 
 def route(cs_ref, ct_ref, take_ref, code_ref, group):
@@ -113,10 +117,11 @@
     code_ref[...] = row
 
 
-def pack(x, take_ref, pay_ref, msg_ref):
+def pack(take_ref, pay_ref, msg_ref):
     got = dot(take_ref[...], pay_ref[...])
     for r in range(CAP):
-        msg_ref[x, pl.ds(r, ND, stride=CAP), :] = got[r * ND : (r + 1) * ND]
+        for x in range(3):
+            msg_ref[x, pl.ds(r, ND, stride=CAP), :] = got[r * ND : (r + 1) * ND, x * LANES : (x + 1) * LANES]
 
 
 def tile_table(pc_ref, sm_ref, table_ref, group):
@@ -149,8 +154,8 @@
     return jnp.where(clear, a, b) + pltpu.roll(jnp.where(clear, b, a), shift, 0)
 
 
-def plane_sums(plane, recv_ref, tile_ref, note_ref, left_ref, right_ref, back_ref):
-    at = pl.multiple_of(plane * LANES, LANES)
+def group_sums(group, recv_ref, tile_ref, note_ref, left_ref, right_ref, back_ref):
+    at = pl.multiple_of(group * LANES, LANES)
     p = [recv_ref[x, pl.ds(at, LANES), :] for x in range(3)]
     tile = [tile_ref[pl.ds(at, LANES), x * LANES : (x + 1) * LANES] for x in range(6)]
     q, n = tile[:3], tile[3:]
@@ -200,13 +205,13 @@
         for level in range(3):
             clear = (sub // (1 << level)) % 2 == 0
             arrays = [fold(arrays[n], arrays[n + 1], clear, 1 << level) for n in range(0, len(arrays), 2)]
-        note = note_ref[pl.ds(plane * 32 + chip * 8, 8), :]
-        back_ref[plane * 4 + chip] = jnp.where((sub % 4 == 3) & (spot < 3), note, arrays[0])
-
-
-def turn(plane, mid_ref, back_ref, turn_ref):
+        note = note_ref[pl.ds(group * 32 + chip * 8, 8), :]
+        back_ref[chip * 4 + low(group - chip + 4, 2)] = jnp.where((sub % 4 == 3) & (spot < 3), note, arrays[0])
+
+
+def turn(plane, partner_ref, source_ref, turn_ref):
     lane = iota((8, LANES), 1)
-    blocks = [mid_ref[plane * 4 + m] for m in range(4)] + [back_ref[plane * 4 + m] for m in range(4)]
+    blocks = [ref[plane * 4 + m] for ref in (partner_ref, source_ref) for m in range(4)]
     for bit in range(3):
         shift = 16 << bit
         clear = (lane // shift) % 2 == 0
@@ -266,32 +271,34 @@
 
 
 def order(p):
-    return 2 * (1 - low(p, 1)) + low(p + high(p, 1), 1)
+    return 2 * high(p, 1) + low(p + high(p, 1), 1)
 
 
 def step_kernel(
-    pc_ref, cs_any, ct_any, src_any, sm_any, block_ref, part_ref,
-    cs_ref, ct_ref, src_ref, sm_ref, take_ref, pay_ref, code_ref, msg_ref, codes_ref, recv_ref, table_ref, tile_ref, note_ref,
-    left_ref, right_ref, back_ref, mid_ref, turn_ref, got_ref, owner_ref, sums_ref, column_ref, lhs_ref,
-    load_sem, send_p, recv_n, recv_p, send_a, recv_a, send_b, recv_b, send_c, recv_c,
+    pc_any, cs_any, ct_any, src_any, sm_any, block_ref, part_ref,
+    pc_ref, cs_ref, ct_ref, src_ref, sm_ref, take_ref, pay_ref, code_ref, msg_ref, codes_ref, recv_ref, table_ref, tile_ref,
+    note_ref, left_ref, right_ref, back_ref, mid_ref, out_ref, in_ref, turn_ref, owner_ref, sums_ref, column_ref, lhs_ref,
+    load_sem, send_n, send_p, recv_n, recv_p, send_a, recv_a, send_b, recv_b, send_c, recv_c,
 ):
     row = lax.axis_index("scan")
     col = lax.axis_index("grp")
     z, y, core = high(row, 3), low(high(row, 1), 2), low(row, 1)
     me = row * NG + col
+    chip = high(row, 1)
+    group = low(y + z, 2)
+    place = group * 32 + z * 8 + core * NG + col
     barrier = pltpu.get_barrier_semaphore()
-
-    @pl.loop(1, ND)
-    def _(step):
-        other = low(me + step, 7)
-        pl.semaphore_signal(barrier, inc=1, device_id=(high(other, 2), low(other, 2)), device_id_type=MESH)
-
     loads = [
         pltpu.make_async_copy(a, b, load_sem.at[n])
         for n, (a, b) in enumerate(
-            [(cs_any, cs_ref), (ct_any, ct_ref), (src_any, src_ref)]
-            + [(sm_any.at[:, x], sm_ref.at[:, x]) for x in range(3)]
-            + [(sm_any.at[:, pl.ds(3, 3)], sm_ref.at[:, pl.ds(3, 3)])]
+            [
+                (cs_any, cs_ref),
+                (ct_any, ct_ref),
+                (src_any, src_ref),
+                (pc_any, pc_ref),
+                (sm_any.at[:, pl.ds(0, 3)], sm_ref.at[:, pl.ds(0, 3)]),
+                (sm_any.at[:, pl.ds(3, 3)], sm_ref.at[:, pl.ds(3, 3)]),
+            ]
         )
     ]
     for load in loads:
@@ -300,74 +307,96 @@
     def to_all(act):
         @pl.loop(0, 16)
         def _(u):
-            uz = low(z + order(high(u, 2)), 2)
-            uy = low(y + order(low(u, 2)), 2)
-            for dc in range(2):
-                for dx in range(NG):
+            dz = low(u + 2, 2)
+            uz = low(z + dz, 2)
+            uy = low(y + order(high(u, 2)) - dz + 4, 2)
+            for dx in (2, 1, 3, 0):
+                for dc in (1, 0):
                     there = ((uz * 4 + uy) * 2 + low(core + dc, 1), low(col + dx, 2))
                     if dc == 0 and dx == 0:
 
-                        @pl.when(u < 15)
+                        @pl.when(u != 2)
                         def _():
                             act(*there)
 
                     else:
                         act(*there)
+
+    to_all(lambda r, c: pl.semaphore_signal(barrier, inc=1, device_id=(r, c), device_id_type=MESH))
 
     def send_codes(r, c):
         pltpu.make_async_remote_copy(
             src_ref=code_ref.at[pl.ds(r * NG + c, 1)],
-            dst_ref=codes_ref.at[pl.ds(me, 1)],
-            send_sem=send_p.at[3],
+            dst_ref=codes_ref.at[pl.ds(place, 1)],
+            send_sem=send_n,
             recv_sem=recv_n,
             device_id=(r, c),
             device_id_type=MESH,
         ).start()
 
-    def send_points(x, r, c):
-        pltpu.make_async_remote_copy(
-            src_ref=msg_ref.at[x, pl.ds((r * NG + c) * CAP, CAP)],
-            dst_ref=recv_ref.at[x, pl.ds(me * CAP, CAP)],
-            send_sem=send_p.at[x],
-            recv_sem=recv_p.at[z],
-            device_id=(r, c),
-            device_id_type=MESH,
-        ).start()
-
-    loads[0].wait()
-    loads[1].wait()
+    def send_points(r, c):
+        for x in range(3):
+            pltpu.make_async_remote_copy(
+                src_ref=msg_ref.at[x, pl.ds((r * NG + c) * CAP, CAP)],
+                dst_ref=recv_ref.at[x, pl.ds(place * CAP, CAP)],
+                send_sem=send_p,
+                recv_sem=recv_p.at[group],
+                device_id=(r, c),
+                device_id_type=MESH,
+            ).start()
+
+    for n in range(5):
+        loads[n].wait()
     route(cs_ref, ct_ref, take_ref, code_ref, col)
-    loads[2].wait()
-    for x in range(3):
-        loads[3 + x].wait()
-        pick_points(x, pc_ref, src_ref, sm_ref, pay_ref.at[x], col)
-        pack(x, take_ref, pay_ref.at[x], msg_ref)
-        if x == 0:
-            pl.semaphore_wait(barrier, ND - 1)
-            pltpu.make_async_copy(code_ref.at[pl.ds(me, 1)], codes_ref.at[pl.ds(me, 1)], recv_n).start()
-            to_all(send_codes)
-        to_all(functools.partial(send_points, x))
+    pick_points(pc_ref, src_ref, sm_ref, pay_ref, col)
+    pack(take_ref, pay_ref, msg_ref)
+    pl.semaphore_wait(barrier, ND - 1)
+    to_all(send_codes)
+    to_all(send_points)
+    pltpu.make_async_copy(code_ref.at[pl.ds(me, 1)], codes_ref.at[pl.ds(place, 1)], recv_n).start()
     pltpu.make_async_copy(
-        msg_ref.at[:, pl.ds(me * CAP, CAP)], recv_ref.at[:, pl.ds(me * CAP, CAP)], recv_p.at[z]
+        msg_ref.at[:, pl.ds(me * CAP, CAP)], recv_ref.at[:, pl.ds(place * CAP, CAP)], recv_p.at[group]
     ).start()
 
-    loads[6].wait()
+    loads[5].wait()
     tile_table(pc_ref, sm_ref, table_ref, col)
     for spot in (7, 10, 11, 12, 13, 14):
         right_ref[:, spot * 16 : (spot + 1) * 16, :] = jnp.zeros((8, 16, 3 * LANES), BF16)
     pltpu.make_async_copy(codes_ref, codes_ref, recv_n).wait()
     fetch_tiles(codes_ref, table_ref, tile_ref, note_ref)
 
+    def cross_all(block_of, which, got, kind):
+        for plane in range(PLANES):
+            at = low(which - plane + 4, 2)
+            src = block_of(plane, at)
+
+            @pl.when(plane != col)
+            def _():
+                pltpu.make_async_remote_copy(
+                    src_ref=src,
+                    dst_ref=got.at[col * 4 + at],
+                    send_sem=send_b.at[kind, plane],
+                    recv_sem=recv_b.at[kind, col],
+                    device_id=(row, plane),
+                    device_id_type=MESH,
+                ).start()
+
+            @pl.when(plane == col)
+            def _():
+                pltpu.make_async_copy(src, got.at[plane * 4 + at], recv_b.at[kind, plane]).start()
+
     @pl.loop(0, PLANES)
     def _(u):
-        plane = low(z + order(u), 2)
-        arrived = recv_ref.at[:, pl.ds(plane * LANES, LANES)]
-        pltpu.make_async_copy(arrived, arrived, recv_p.at[plane]).wait()
-        plane_sums(plane, recv_ref, tile_ref, note_ref, left_ref, right_ref, back_ref)
+        which = low(group - order(u) + 4, 2)
+        arrived = recv_ref.at[:, pl.ds(which * LANES, LANES)]
+        pltpu.make_async_copy(arrived, arrived, recv_p.at[which]).wait()
+        group_sums(which, recv_ref, tile_ref, note_ref, left_ref, right_ref, back_ref)
         for n in range(8):
-            to_row = plane * 8 + n
-            src = back_ref.at[plane * 4 + n // 2, pl.ds(n % 2 * 4, 4)]
-            dst = mid_ref.at[high(row, 1), pl.ds(core * 4, 4)]
+            to_z = n // 2
+            to_chip = to_z * 4 + low(which - to_z + 4, 2)
+            to_row = to_chip * 2 + n % 2
+            src = back_ref.at[to_chip, pl.ds(n % 2 * 4, 4)]
+            dst = mid_ref.at[group * 4 + z, pl.ds(core * 4, 4)]
 
             @pl.when(to_row != row)
             def _():
@@ -375,26 +404,23 @@
                     src_ref=src,
                     dst_ref=dst,
                     send_sem=send_a,
-                    recv_sem=recv_a,
+                    recv_sem=recv_a.at[group],
                     device_id=(to_row, col),
                     device_id_type=MESH,
                 ).start()
 
             @pl.when(to_row == row)
             def _():
-                pltpu.make_async_copy(src, dst, recv_a).start()
-
-    pltpu.make_async_copy(mid_ref, mid_ref, recv_a).wait()
-
-    def give(to_col, at):
-        return pltpu.make_async_remote_copy(
-            src_ref=turn_ref.at[to_col],
-            dst_ref=got_ref.at[at],
-            send_sem=send_b.at[to_col],
-            recv_sem=recv_b.at[at],
-            device_id=(row, to_col),
-            device_id_type=MESH,
-        )
+                pltpu.make_async_copy(src, dst, recv_a.at[group]).start()
+
+        cross_all(lambda plane, at: back_ref.at[plane * 4 + at], which, in_ref, 0)
+
+    @pl.loop(0, PLANES)
+    def _(u):
+        which = low(group + order(u), 2)
+        arrived = mid_ref.at[pl.ds(which * 4, 4)]
+        pltpu.make_async_copy(arrived, arrived, recv_a.at[which]).wait()
+        cross_all(lambda plane, at: mid_ref.at[which * 4 + plane], which, out_ref, 1)
 
     def spread(to_col, at):
         return pltpu.make_async_remote_copy(
@@ -408,32 +434,31 @@
 
     for plane in range(PLANES):
         turn(plane, mid_ref, back_ref, turn_ref)
-    for step in (2, 1, 3):
-        give(low(col + step, 2), col).start()
-    own = pltpu.make_async_copy(turn_ref.at[col], got_ref.at[col], recv_b.at[col])
-    own.start()
     arrange(turn_ref, owner_ref, sums_ref, None)
     part_ref[col] = scan_sums(owner_ref, sums_ref)
     for step in (2, 1, 3):
         spread(low(col + step, 2), col).start()
 
-    for x in range(3):
-        left = msg_ref.at[x, pl.ds(0, (ND - 1) * CAP)]
-        pltpu.make_async_copy(left, left, send_p.at[x]).wait()
     left = code_ref.at[pl.ds(0, ND - 1)]
-    pltpu.make_async_copy(left, left, send_p.at[3]).wait()
+    pltpu.make_async_copy(left, left, send_n).wait()
+    left = msg_ref.at[:, pl.ds(0, (ND - 1) * CAP)]
+    pltpu.make_async_copy(left, left, send_p).wait()
     for left in (back_ref.at[pl.ds(0, 15)], back_ref.at[15, pl.ds(0, 4)]):
         pltpu.make_async_copy(left, left, send_a).wait()
 
-    own.wait()
-    for step in range(1, NG):
-        other = low(col + step, 2)
-        give(other, other).wait_recv()
-    arrange(got_ref, owner_ref, sums_ref, column_ref)
+    for kind, got in enumerate((in_ref, out_ref)):
+        for source in range(NG):
+            arrived = got.at[pl.ds(source * 4, 4)]
+            pltpu.make_async_copy(arrived, arrived, recv_b.at[kind, source]).wait()
+    for plane in range(PLANES):
+        turn(plane, out_ref, in_ref, turn_ref)
+    arrange(turn_ref, owner_ref, sums_ref, column_ref)
     matrix(owner_ref, sums_ref, column_ref, lhs_ref, block_ref)
     for step in range(1, NG):
         other = low(col + step, 2)
-        give(other, col).wait_send()
+        for kind in range(2):
+            left = back_ref.at[pl.ds(0, 4)]
+            pltpu.make_async_copy(left, left, send_b.at[kind, other]).wait()
         spread(other, col).wait_send()
         spread(other, other).wait_recv()
 
@@ -472,15 +497,16 @@
             jax.ShapeDtypeStruct((len(PAIRS) * LOC, LANES), F32),
             jax.ShapeDtypeStruct((NG, LOC, LANES), F32),
         ),
-        in_specs=[pl.BlockSpec(memory_space=pltpu.SMEM)] + [pl.BlockSpec(memory_space=pl.ANY)] * 4,
+        in_specs=[pl.BlockSpec(memory_space=pl.ANY)] * 5,
         out_specs=tuple(vmem(2)),
         scratch_shapes=[
+            pltpu.SMEM((LOC,), I32),
             pltpu.VMEM((LOC, CT), I32),
             pltpu.VMEM((LOC, CT), I32),
             pltpu.VMEM((LOC, CT, LANES), I32),
             pltpu.VMEM((LOC, 6, TL, LANES), F32),
             pltpu.VMEM((SLOTS, 3 * REQ), BF16),
-            pltpu.VMEM((3, 3 * REQ, LANES), BF16),
+            pltpu.VMEM((3 * REQ, 3 * LANES), BF16),
             pltpu.VMEM((ND, LANES), F32),
             pltpu.VMEM((3, SLOTS, LANES), F32),
             pltpu.VMEM((ND, LANES), F32),
@@ -492,20 +518,22 @@
             pltpu.VMEM((8, 16 * 16, 3 * LANES), BF16),
             pltpu.VMEM((16, 8, LANES), F32),
             pltpu.VMEM((16, 8, LANES), F32),
+            pltpu.VMEM((16, 8, LANES), F32),
+            pltpu.VMEM((16, 8, LANES), F32),
             pltpu.VMEM((PLANES, 8, 8, LANES), F32),
-            pltpu.VMEM((NG, 8, 8, LANES), F32),
             pltpu.VMEM((LOC, 2 * HALF), BF16),
             pltpu.VMEM((64, 2 * HALF), BF16),
             pltpu.VMEM((LANES, 4 * HALF), BF16),
             pltpu.VMEM((len(PAIRS) * LOC, 4 * HALF), BF16),
-            dma((7,)),
-            dma((4,)),
+            dma((6,)),
+            dma,
+            dma,
             dma,
             dma((PLANES,)),
             dma,
-            dma,
-            dma((NG,)),
-            dma((NG,)),
+            dma((PLANES,)),
+            dma((2, NG)),
+            dma((2, NG)),
             dma((NG,)),
             dma((NG,)),
         ],

time: 39.8 us -> 36.6 us (0.920)
  Pallas kernels: 39 us -> 35.8 us
    pallas_call x1, Pallas kernels: 37.1 us -> 34 us  [local(): pl.pallas_call(step_kernel, out_shape=(jax.ShapeDtypeStruct((len(PAIRS) *...]
where the time goes in v6:
time: 36.6 us; the launch traced here: 36.5 us
  Pallas kernels  35.8 us (98%)
  between operations  0.64 us (2%)
    pallas_call x1, Pallas kernels, local(): pl.pallas_call(step_kernel, out_shape=(jax.ShapeDtypeStruct((len(PAIRS) *...  34 us
    pallas_call x1, Pallas kernels, local(): pl.pallas_call(finish_kernel, out_shape=(jax.ShapeDtypeStruct((6, 6, LOC,...  1.85 us

profile of v6, /device:TPU:1, one launch (start us, length us, event | category | flops | bytes accessed | tf_op | source)
XLA Modules:
  0.0 36.5 jit_solution(12641518529960002767)
XLA Ops:
  0.6 34.0 %step.1 = (f32[336,128]{1,0:T(8,128)}, f32[4,16,128]{2,1,0:T(8,128)}) custom-call(s32[16]{0:T(128)} %pc_any.1, s32[16,16]{1,0:T(8,128)} %cs_any.1, s32[16,16]{1,0:T(8,128)} %ct_any.1, s32[16,16,128]{2,1,0:T(8,128)} %src_any.1, f32[16,6,16,128]{3,2,1,0:T(8,128)} %bitcast.2), custom_call_target="tpu_custom_call" | custom-call | tf_op jit(solution)/shard_map/step/pallas_call | solution.py:494
  34.6 1.8 %finish.1 = (f32[6,6,16,128]{3,2,1,0:T(8,128)}, f32[4,6]{1,0:T(4,128)}) custom-call(f32[336,128]{1,0:T(8,128)} %get-tuple-element.6.block_ref, f32[4,16,128]{2,1,0:T(8,128)} %get-tuple-element.7.part_ref), custom_call_target="tpu_custom_call" | custom-call | tf_op jit(solution)/shard_map/finish/pallas_call | solution.py:543

commit v7 on v6

--- a/solution.py
+++ b/solution.py
@@ -209,9 +209,8 @@
         back_ref[chip * 4 + low(group - chip + 4, 2)] = jnp.where((sub % 4 == 3) & (spot < 3), note, arrays[0])
 
 
-def turn(plane, partner_ref, source_ref, turn_ref):
+def turn(blocks, signs, turn_ref, at):
     lane = iota((8, LANES), 1)
-    blocks = [ref[plane * 4 + m] for ref in (partner_ref, source_ref) for m in range(4)]
     for bit in range(3):
         shift = 16 << bit
         clear = (lane // shift) % 2 == 0
@@ -221,36 +220,38 @@
                 blocks[m] = jnp.where(clear, a, pltpu.roll(b, shift, 1))
                 blocks[m + (1 << bit)] = jnp.where(clear, pltpu.roll(a, LANES - shift, 1), b)
     for n in range(8):
-        turn_ref[plane, n] = jnp.where(lane < 64, blocks[n], -blocks[n]) if n >= 6 else blocks[n]
-
-
-def arrange(turn_ref, owner_ref, sums_ref, column_ref):
+        turn_ref[at, n] = jnp.where(lane < 64, blocks[n], -blocks[n]) if signs and n >= 6 else blocks[n]
+
+
+def arrange(turn_ref, count, signs, owner_ref, sums_ref, column_ref):
     lane = iota((1, LANES), 1)
     y = (lane // 16) % 4
-    for t in range(PLANES):
+    half = count * LANES
+    for t in range(count):
         source = turn_ref[t, 0]
         target = turn_ref[t, 1]
         for c in range(2):
             s = source[c * 4 + 3 : c * 4 + 4, :]
             b = target[c * 4 + 3 : c * 4 + 4, :]
-            owner = jnp.broadcast_to(jnp.where(lane < 64, s, b), (LOC, LANES))
-            at = c * HALF + t * LANES
+            owner = jnp.broadcast_to(jnp.where(lane < 64, s, b) if signs else s, (LOC, LANES))
+            at = c * half + t * LANES
             owner_ref[:, at : at + LANES] = onehot(owner == iota((LOC, LANES), 0).astype(F32))
             if column_ref is not None:
                 column = jnp.where(lane < 64, b, s) + (16 * (2 * y + c)).astype(F32)
                 there = jnp.broadcast_to(column, (LANES, LANES)) == iota((LANES, LANES), 0).astype(F32)
                 there = jnp.where(there, -1.0, 0.0).astype(BF16)
                 for n in range(2):
-                    column_ref[:, n * 2 * HALF + at : n * 2 * HALF + at + LANES] = there
+                    column_ref[:, n * 2 * half + at : n * 2 * half + at + LANES] = there
         for p in range(0, 8, 2):
             pair = jnp.concatenate([turn_ref[t, p], turn_ref[t, p + 1]], axis=0)
             for n, term in enumerate(parts_of(pair, 2)):
-                sums_ref[p * 8 : p * 8 + 16, n * HALF + t * LANES : n * HALF + (t + 1) * LANES] = term
-
-
-def scan_sums(owner_ref, sums_ref):
-    owners = [jnp.concatenate([owner_ref[:, c * HALF : (c + 1) * HALF]] * 2, axis=1) for c in range(2)]
-    both = dot_t(jnp.concatenate(owners, axis=0), sums_ref[...])
+                sums_ref[p * 8 : p * 8 + 16, n * half + t * LANES : n * half + (t + 1) * LANES] = term
+
+
+def scan_sums(count, owner_ref, sums_ref):
+    half = count * LANES
+    owners = [jnp.concatenate([owner_ref[:, c * half : (c + 1) * half]] * 2, axis=1) for c in range(2)]
+    both = dot_t(jnp.concatenate(owners, axis=0), sums_ref[:, : 2 * half])
     lane = iota((LOC, 64), 1)
     part = jnp.where((lane // 4) % 2 == 0, both[:LOC], both[LOC:])
     return jnp.concatenate([part, jnp.zeros((LOC, LANES - 64), F32)], axis=1)
@@ -270,6 +271,10 @@
     block_ref[...] = dot_t(lhs_ref[...], column_ref[...])
 
 
+def far(p):
+    return 2 * (1 - low(p, 1)) + low(p + high(p, 1), 1)
+
+
 def order(p):
     return 2 * high(p, 1) + low(p + high(p, 1), 1)
 
@@ -277,8 +282,8 @@
 def step_kernel(
     pc_any, cs_any, ct_any, src_any, sm_any, block_ref, part_ref,
     pc_ref, cs_ref, ct_ref, src_ref, sm_ref, take_ref, pay_ref, code_ref, msg_ref, codes_ref, recv_ref, table_ref, tile_ref,
-    note_ref, left_ref, right_ref, back_ref, mid_ref, out_ref, in_ref, turn_ref, owner_ref, sums_ref, column_ref, lhs_ref,
-    load_sem, send_n, send_p, recv_n, recv_p, send_a, recv_a, send_b, recv_b, send_c, recv_c,
+    note_ref, left_ref, right_ref, back_ref, mid_ref, out_ref, in_ref, last_ref, turn_ref, owner_ref, sums_ref, column_ref, lhs_ref,
+    load_sem, send_n, send_p, recv_n, recv_p, send_a, recv_a, send_l, recv_l, send_b, recv_b, send_c, recv_c,
 ):
     row = lax.axis_index("scan")
     col = lax.axis_index("grp")
@@ -304,8 +309,8 @@
     for load in loads:
         load.start()
 
-    def to_all(act):
-        @pl.loop(0, 16)
+    def to_some(first, last, act):
+        @pl.loop(first, last)
         def _(u):
             dz = low(u + 2, 2)
             uz = low(z + dz, 2)
@@ -322,7 +327,22 @@
                     else:
                         act(*there)
 
-    to_all(lambda r, c: pl.semaphore_signal(barrier, inc=1, device_id=(r, c), device_id_type=MESH))
+    @pl.loop(0, 16)
+    def _(u):
+        far_z = low(z + far(high(u, 2)), 2)
+        far_y = low(y + far(low(u, 2)), 2)
+        for dx in (2, 1, 3, 0):
+            for dc in (1, 0):
+
+                def greet():
+                    there = ((far_z * 4 + far_y) * 2 + low(core + dc, 1), low(col + dx, 2))
+                    pl.semaphore_signal(barrier, inc=1, device_id=there, device_id_type=MESH)
+
+                if dc == 0 and dx == 0:
+                    pl.when(u < 15)(greet)
+                else:
+                    greet()
+
 
     def send_codes(r, c):
         pltpu.make_async_remote_copy(
@@ -351,8 +371,9 @@
     pick_points(pc_ref, src_ref, sm_ref, pay_ref, col)
     pack(take_ref, pay_ref, msg_ref)
     pl.semaphore_wait(barrier, ND - 1)
-    to_all(send_codes)
-    to_all(send_points)
+    to_some(0, 4, send_points)
+    to_some(0, 16, send_codes)
+    to_some(4, 16, send_points)
     pltpu.make_async_copy(code_ref.at[pl.ds(me, 1)], codes_ref.at[pl.ds(place, 1)], recv_n).start()
     pltpu.make_async_copy(
         msg_ref.at[:, pl.ds(me * CAP, CAP)], recv_ref.at[:, pl.ds(place * CAP, CAP)], recv_p.at[group]
@@ -385,12 +406,16 @@
             def _():
                 pltpu.make_async_copy(src, got.at[plane * 4 + at], recv_b.at[kind, plane]).start()
 
-    @pl.loop(0, PLANES)
-    def _(u):
+    def serve(u):
         which = low(group - order(u) + 4, 2)
         arrived = recv_ref.at[:, pl.ds(which * LANES, LANES)]
         pltpu.make_async_copy(arrived, arrived, recv_p.at[which]).wait()
         group_sums(which, recv_ref, tile_ref, note_ref, left_ref, right_ref, back_ref)
+        return which
+
+    @pl.loop(0, PLANES - 1)
+    def _(u):
+        which = serve(u)
         for n in range(8):
             to_z = n // 2
             to_chip = to_z * 4 + low(which - to_z + 4, 2)
@@ -415,7 +440,22 @@
 
         cross_all(lambda plane, at: back_ref.at[plane * 4 + at], which, in_ref, 0)
 
-    @pl.loop(0, PLANES)
+    which = serve(PLANES - 1)
+    for n in range(8):
+        to_z = n // 2
+        to_chip = to_z * 4 + low(which - to_z + 4, 2)
+        for step in (2, 1, 3, 0):
+            pltpu.make_async_remote_copy(
+                src_ref=back_ref.at[to_chip, pl.ds(n % 2 * 4, 4)],
+                dst_ref=last_ref.at[col * 4 + z, pl.ds(core * 4, 4)],
+                send_sem=send_l,
+                recv_sem=recv_l,
+                device_id=(to_chip * 2 + n % 2, low(col + step, 2)),
+                device_id_type=MESH,
+            ).start()
+    cross_all(lambda plane, at: back_ref.at[plane * 4 + at], which, in_ref, 0)
+
+    @pl.loop(0, PLANES - 1)
     def _(u):
         which = low(group + order(u), 2)
         arrived = mid_ref.at[pl.ds(which * 4, 4)]
@@ -432,10 +472,13 @@
             device_id_type=MESH,
         )
 
-    for plane in range(PLANES):
-        turn(plane, mid_ref, back_ref, turn_ref)
-    arrange(turn_ref, owner_ref, sums_ref, None)
-    part_ref[col] = scan_sums(owner_ref, sums_ref)
+    late = low(group + order(PLANES - 1), 2)
+    for m in range(4):
+        mid_ref[late * 4 + m] = jnp.zeros((8, LANES), F32)
+    for t in range(PLANES):
+        turn([ref[t * 4 + m] for ref in (mid_ref, back_ref) for m in range(4)], True, turn_ref, t)
+    arrange(turn_ref, PLANES, True, owner_ref, sums_ref, None)
+    part_ref[col] = scan_sums(PLANES, owner_ref, sums_ref)
     for step in (2, 1, 3):
         spread(low(col + step, 2), col).start()
 
@@ -443,21 +486,30 @@
     pltpu.make_async_copy(left, left, send_n).wait()
     left = msg_ref.at[:, pl.ds(0, (ND - 1) * CAP)]
     pltpu.make_async_copy(left, left, send_p).wait()
-    for left in (back_ref.at[pl.ds(0, 15)], back_ref.at[15, pl.ds(0, 4)]):
+    for left in (back_ref.at[pl.ds(0, 11)], back_ref.at[11, pl.ds(0, 4)]):
         pltpu.make_async_copy(left, left, send_a).wait()
-
-    for kind, got in enumerate((in_ref, out_ref)):
-        for source in range(NG):
-            arrived = got.at[pl.ds(source * 4, 4)]
-            pltpu.make_async_copy(arrived, arrived, recv_b.at[kind, source]).wait()
-    for plane in range(PLANES):
-        turn(plane, out_ref, in_ref, turn_ref)
-    arrange(turn_ref, owner_ref, sums_ref, column_ref)
+    pltpu.make_async_copy(last_ref, last_ref, send_l).wait()
+
+    for source in range(NG):
+        arrived = in_ref.at[pl.ds(source * 4, 4)]
+        pltpu.make_async_copy(arrived, arrived, recv_b.at[0, source]).wait()
+        arrived = out_ref.at[pl.ds(source * 4, 3)]
+        pltpu.make_async_copy(arrived, arrived, recv_b.at[1, source]).wait()
+    pltpu.make_async_copy(last_ref, last_ref, recv_l).wait()
+    for t in range(PLANES):
+        out_ref[t * 4 + low(late - col + 4, 2)] = last_ref[t * 4 + col]
+    for t in range(2):
+        turn([last_ref[t * 8 + m] for m in range(8)], False, turn_ref, t)
+    arrange(turn_ref, 2, False, owner_ref, sums_ref, None)
+    part_ref[NG] = scan_sums(2, owner_ref, sums_ref)
+    for t in range(PLANES):
+        turn([ref[t * 4 + m] for ref in (out_ref, in_ref) for m in range(4)], True, turn_ref, t)
+    arrange(turn_ref, PLANES, True, owner_ref, sums_ref, column_ref)
     matrix(owner_ref, sums_ref, column_ref, lhs_ref, block_ref)
     for step in range(1, NG):
         other = low(col + step, 2)
         for kind in range(2):
-            left = back_ref.at[pl.ds(0, 4)]
+            left = back_ref.at[pl.ds(0, 4 - kind)]
             pltpu.make_async_copy(left, left, send_b.at[kind, other]).wait()
         spread(other, col).wait_send()
         spread(other, other).wait_recv()
@@ -466,7 +518,7 @@
 def finish_kernel(block_ref, part_ref, hess_ref, grad_ref):
     row = lax.axis_index("scan")
     col = lax.axis_index("grp")
-    total = part_ref[0] + part_ref[1] + part_ref[2] + part_ref[3]
+    total = part_ref[0] + part_ref[1] + part_ref[2] + part_ref[3] + part_ref[4]
     total = total + pltpu.roll(total, LANES - 4, 1)
     lane = iota((LOC, LANES), 1)
     diag = (lane == iota((LOC, LANES), 0) + LOC * (row % 8)) & (row // 8 == col)
@@ -494,8 +546,8 @@
     block, parts = pl.pallas_call(
         step_kernel,
         out_shape=(
-            jax.ShapeDtypeStruct((len(PAIRS) * LOC, LANES), F32),
-            jax.ShapeDtypeStruct((NG, LOC, LANES), F32),
+            pltpu.VMEM((len(PAIRS) * LOC, LANES), F32),
+            pltpu.VMEM((NG + 1, LOC, LANES), F32),
         ),
         in_specs=[pl.BlockSpec(memory_space=pl.ANY)] * 5,
         out_specs=tuple(vmem(2)),
@@ -520,6 +572,7 @@
             pltpu.VMEM((16, 8, LANES), F32),
             pltpu.VMEM((16, 8, LANES), F32),
             pltpu.VMEM((16, 8, LANES), F32),
+            pltpu.VMEM((16, 8, LANES), F32),
             pltpu.VMEM((PLANES, 8, 8, LANES), F32),
             pltpu.VMEM((LOC, 2 * HALF), BF16),
             pltpu.VMEM((64, 2 * HALF), BF16),
@@ -532,6 +585,8 @@
             dma((PLANES,)),
             dma,
             dma((PLANES,)),
+            dma,
+            dma,
             dma((2, NG)),
             dma((2, NG)),
             dma((NG,)),
@@ -548,6 +603,7 @@
         ),
         in_specs=vmem(2),
         out_specs=tuple(vmem(2)),
+        compiler_params=pltpu.CompilerParams(vmem_limit_bytes=8 * 1024 * 1024),
         name="finish",
     )(block, parts)
     return hessian.transpose(2, 0, 1, 3), gradient

time: 36.6 us -> 33.4 us (0.913)
  Pallas kernels: 35.8 us -> 32.7 us
    pallas_call x1, Pallas kernels: 34 us -> 31.7 us  [local(): pl.pallas_call(step_kernel, out_shape=(pltpu.VMEM((len(PAIRS) * LOC, LANE...]
    pallas_call x1, Pallas kernels: 1.85 us -> 0.93 us  [local(): pl.pallas_call(finish_kernel, out_shape=(jax.ShapeDtypeStruct((6, 6, LOC,...]
where the time goes in v7:
time: 33.4 us; the launch traced here: 33.3 us
  Pallas kernels  32.7 us (98%)
  between operations  0.64 us (2%)
    pallas_call x1, Pallas kernels, local(): pl.pallas_call(step_kernel, out_shape=(pltpu.VMEM((len(PAIRS) * LOC, LANE...  31.7 us
    pallas_call x1, Pallas kernels, local(): pl.pallas_call(finish_kernel, out_shape=(jax.ShapeDtypeStruct((6, 6, LOC,...  0.93 us

profile of v7, /device:TPU:1, one launch (start us, length us, event | category | flops | bytes accessed | tf_op | source)
XLA Modules:
  0.0 33.3 jit_solution(3062012571790780346)
XLA Ops:
  0.6 31.7 %step.1 = (f32[336,128]{1,0:T(8,128)S(1)}, f32[5,16,128]{2,1,0:T(8,128)S(1)}) custom-call(s32[16]{0:T(128)} %pc_any.1, s32[16,16]{1,0:T(8,128)} %cs_any.1, s32[16,16]{1,0:T(8,128)} %ct_any.1, s32[16,16,128]{2,1,0:T(8,128)} %src_any.1, f32[16,6,16,128]{3,2,1,0:T(8,128)} %bitcast.2), custom_call_target="tpu_custom_call" | custom-call | tf_op jit(solution)/shard_map/step/pallas_call | solution.py:546
  32.4 0.9 %finish.1 = (f32[6,6,16,128]{3,2,1,0:T(8,128)}, f32[4,6]{1,0:T(4,128)}) custom-call(f32[336,128]{1,0:T(8,128)S(1)} %get-tuple-element.6.block_ref, f32[5,16,128]{2,1,0:T(8,128)S(1)} %get-tuple-element.7.part_ref), custom_call_target="tpu_custom_call" | custom-call | tf_op jit(solution)/shard_map/finish/pallas_call | solution.py:598

commit v8 on v7

--- a/solution.py
+++ b/solution.py
@@ -312,7 +312,7 @@
     def to_some(first, last, act):
         @pl.loop(first, last)
         def _(u):
-            dz = low(u + 2, 2)
+            dz = low(u + 2 + 2 * core + col, 2)
             uz = low(z + dz, 2)
             uy = low(y + order(high(u, 2)) - dz + 4, 2)
             for dx in (2, 1, 3, 0):
@@ -320,7 +320,7 @@
                     there = ((uz * 4 + uy) * 2 + low(core + dc, 1), low(col + dx, 2))
                     if dc == 0 and dx == 0:
 
-                        @pl.when(u != 2)
+                        @pl.when(jnp.logical_or(u >= 4, dz != 0))
                         def _():
                             act(*there)
 

time: 33.4 us -> 33 us (0.988)
  Pallas kernels: 32.7 us -> 32.2 us
    pallas_call x1, Pallas kernels: 31.7 us -> 31.3 us  [local(): pl.pallas_call(step_kernel, out_shape=(pltpu.VMEM((len(PAIRS) * LOC, LANE...]
where the time goes in v8:
time: 33 us; the launch traced here: 32.9 us
  Pallas kernels  32.2 us (98%)
  between operations  0.64 us (2%)
    pallas_call x1, Pallas kernels, local(): pl.pallas_call(step_kernel, out_shape=(pltpu.VMEM((len(PAIRS) * LOC, LANE...  31.3 us
    pallas_call x1, Pallas kernels, local(): pl.pallas_call(finish_kernel, out_shape=(jax.ShapeDtypeStruct((6, 6, LOC,...  0.93 us

profile of v8, /device:TPU:1, one launch (start us, length us, event | category | flops | bytes accessed | tf_op | source)
XLA Modules:
  0.0 32.9 jit_solution(6183989572706788204)
XLA Ops:
  0.6 31.3 %step.1 = (f32[336,128]{1,0:T(8,128)S(1)}, f32[5,16,128]{2,1,0:T(8,128)S(1)}) custom-call(s32[16]{0:T(128)} %pc_any.1, s32[16,16]{1,0:T(8,128)} %cs_any.1, s32[16,16]{1,0:T(8,128)} %ct_any.1, s32[16,16,128]{2,1,0:T(8,128)} %src_any.1, f32[16,6,16,128]{3,2,1,0:T(8,128)} %bitcast.2), custom_call_target="tpu_custom_call" | custom-call | tf_op jit(solution)/shard_map/step/pallas_call | solution.py:546
  31.9 0.9 %finish.1 = (f32[6,6,16,128]{3,2,1,0:T(8,128)}, f32[4,6]{1,0:T(4,128)}) custom-call(f32[336,128]{1,0:T(8,128)S(1)} %get-tuple-element.6.block_ref, f32[5,16,128]{2,1,0:T(8,128)S(1)} %get-tuple-element.7.part_ref), custom_call_target="tpu_custom_call" | custom-call | tf_op jit(solution)/shard_map/finish/pallas_call | solution.py:598

commit v9 on v8

--- a/solution.py
+++ b/solution.py
@@ -515,7 +515,7 @@
         spread(other, other).wait_recv()
 
 
-def finish_kernel(block_ref, part_ref, hess_ref, grad_ref):
+def finish_kernel(block_ref, part_ref, hess_any, grad_ref, hess_ref, sem):
     row = lax.axis_index("scan")
     col = lax.axis_index("grp")
     total = part_ref[0] + part_ref[1] + part_ref[2] + part_ref[3] + part_ref[4]
@@ -530,11 +530,15 @@
         hess_ref[i, j] = value
         if i != j:
             hess_ref[j, i] = value
+        if j == 5:
+            pltpu.make_async_copy(hess_ref.at[i], hess_any.at[i], sem.at[i]).start()
     some = jnp.zeros((4, LANES), F32)
     for n in range(NG):
         some = jnp.where(col == n, total[n * 4 : (n + 1) * 4, :], some)
     at = [SPOT[i, 6][1] * 8 + SPOT[i, 6][0] for i in range(6)]
     grad_ref[...] = jnp.concatenate([some[:, a : a + 1] for a in at], axis=1)
+    for i in range(6):
+        pltpu.make_async_copy(hess_ref.at[i], hess_any.at[i], sem.at[i]).wait()
 
 
 def vmem(count):
@@ -602,7 +606,8 @@
             jax.ShapeDtypeStruct((4, 6), F32),
         ),
         in_specs=vmem(2),
-        out_specs=tuple(vmem(2)),
+        out_specs=(pl.BlockSpec(memory_space=pl.ANY), *vmem(1)),
+        scratch_shapes=[pltpu.VMEM((6, 6, LOC, LANES), F32), pltpu.SemaphoreType.DMA((6,))],
         compiler_params=pltpu.CompilerParams(vmem_limit_bytes=8 * 1024 * 1024),
         name="finish",
     )(block, parts)

time: 33 us -> 33.5 us (1.015)
  Pallas kernels: 32.2 us -> 32.8 us
    pallas_call x1, Pallas kernels: 0.93 us -> 1.49 us  [local(): pl.pallas_call(finish_kernel, out_shape=(jax.ShapeDtypeStruct((6, 6, LOC,...]
where the time goes in v9:
time: 33.5 us; the launch traced here: 33.4 us
  Pallas kernels  32.8 us (98%)
  between operations  0.64 us (2%)
    pallas_call x1, Pallas kernels, local(): pl.pallas_call(step_kernel, out_shape=(pltpu.VMEM((len(PAIRS) * LOC, LANE...  31.3 us
    pallas_call x1, Pallas kernels, local(): pl.pallas_call(finish_kernel, out_shape=(jax.ShapeDtypeStruct((6, 6, LOC,...  1.49 us

profile of v9, /device:TPU:1, one launch (start us, length us, event | category | flops | bytes accessed | tf_op | source)
XLA Modules:
  0.0 33.4 jit_solution(14177399086114388195)
XLA Ops:
  0.6 31.3 %step.1 = (f32[336,128]{1,0:T(8,128)S(1)}, f32[5,16,128]{2,1,0:T(8,128)S(1)}) custom-call(s32[16]{0:T(128)} %pc_any.1, s32[16,16]{1,0:T(8,128)} %cs_any.1, s32[16,16]{1,0:T(8,128)} %ct_any.1, s32[16,16,128]{2,1,0:T(8,128)} %src_any.1, f32[16,6,16,128]{3,2,1,0:T(8,128)} %bitcast.2), custom_call_target="tpu_custom_call" | custom-call | tf_op jit(solution)/shard_map/step/pallas_call | solution.py:550
  31.9 1.5 %finish.1 = (f32[6,6,16,128]{3,2,1,0:T(8,128)}, f32[4,6]{1,0:T(4,128)}) custom-call(f32[336,128]{1,0:T(8,128)S(1)} %get-tuple-element.6.block_ref, f32[5,16,128]{2,1,0:T(8,128)S(1)} %get-tuple-element.7.part_ref), custom_call_target="tpu_custom_call" | custom-call | tf_op jit(solution)/shard_map/finish/pallas_call | solution.py:602

commit v10 on v8

--- a/solution.py
+++ b/solution.py
@@ -312,7 +312,7 @@
     def to_some(first, last, act):
         @pl.loop(first, last)
         def _(u):
-            dz = low(u + 2 + 2 * core + col, 2)
+            dz = low(u + 2 + core + col, 2)
             uz = low(z + dz, 2)
             uy = low(y + order(high(u, 2)) - dz + 4, 2)
             for dx in (2, 1, 3, 0):

time: 33 us -> 32.9 us (level)
  no operation moved by 1% of the time
where the time goes in v10:
time: 32.9 us; the launch traced here: 32.8 us
  Pallas kernels  32.2 us (98%)
  between operations  0.64 us (2%)
    pallas_call x1, Pallas kernels, local(): pl.pallas_call(step_kernel, out_shape=(pltpu.VMEM((len(PAIRS) * LOC, LANE...  31.2 us
    pallas_call x1, Pallas kernels, local(): pl.pallas_call(finish_kernel, out_shape=(jax.ShapeDtypeStruct((6, 6, LOC,...  0.93 us

profile of v10, /device:TPU:1, one launch (start us, length us, event | category | flops | bytes accessed | tf_op | source)
XLA Modules:
  0.0 32.8 jit_solution(7769744688563631626)
XLA Ops:
  0.6 31.2 %step.1 = (f32[336,128]{1,0:T(8,128)S(1)}, f32[5,16,128]{2,1,0:T(8,128)S(1)}) custom-call(s32[16]{0:T(128)} %pc_any.1, s32[16,16]{1,0:T(8,128)} %cs_any.1, s32[16,16]{1,0:T(8,128)} %ct_any.1, s32[16,16,128]{2,1,0:T(8,128)} %src_any.1, f32[16,6,16,128]{3,2,1,0:T(8,128)} %bitcast.2), custom_call_target="tpu_custom_call" | custom-call | tf_op jit(solution)/shard_map/step/pallas_call | solution.py:546
  31.9 0.9 %finish.1 = (f32[6,6,16,128]{3,2,1,0:T(8,128)}, f32[4,6]{1,0:T(4,128)}) custom-call(f32[336,128]{1,0:T(8,128)S(1)} %get-tuple-element.6.block_ref, f32[5,16,128]{2,1,0:T(8,128)S(1)} %get-tuple-element.7.part_ref), custom_call_target="tpu_custom_call" | custom-call | tf_op jit(solution)/shard_map/finish/pallas_call | solution.py:598
